TPU v7x, 32 devices: a whole 2x2x4 slice. The times are simulated.
32 devices in a mesh: stage: 4 (over x, y), data: 8 (over z, core).
Axes of the slice: x: 2, y: 2, z: 4, core: 2. Of those that a mesh axis runs over, the one named last changes fastest.
Arguments:
- w_qkv: float32 [12, 1024, 2048], P('stage', 'data'), parts along dimension 0
- m_qkv: float32 [12, 1024, 2048], P('stage', 'data'), parts along dimension 0
- g_qkv: bfloat16 [12, 1024, 2048], P('stage', 'data'), parts along dimension 0
- w_out: float32 [12, 1024, 1024], P('stage', 'data'), parts along dimension 0
- m_out: float32 [12, 1024, 1024], P('stage', 'data'), parts along dimension 0
- g_out: bfloat16 [12, 1024, 1024], P('stage', 'data'), parts along dimension 0
- w_up: float32 [48, 1024, 512], P('stage', 'data'), parts along dimension 0
- m_up: float32 [48, 1024, 512], P('stage', 'data'), parts along dimension 0
- g_up: bfloat16 [48, 1024, 512], P('stage', 'data'), parts along dimension 0
- w_down: float32 [48, 512, 1024], P('stage', 'data'), parts along dimension 0
- m_down: float32 [48, 512, 1024], P('stage', 'data'), parts along dimension 0
- g_down: bfloat16 [48, 512, 1024], P('stage', 'data'), parts along dimension 0
Outputs:
- output 1: float32 [12, 1024, 2048], P('stage', 'data'), parts along dimension 0
- output 2: float32 [12, 1024, 2048], P('stage', 'data'), parts along dimension 0
- output 3: float32 [12, 1024, 1024], P('stage', 'data'), parts along dimension 0
- output 4: float32 [12, 1024, 1024], P('stage', 'data'), parts along dimension 0
- output 5: float32 [48, 1024, 512], P('stage', 'data'), parts along dimension 0
- output 6: float32 [48, 1024, 512], P('stage', 'data'), parts along dimension 0
- output 7: float32 [48, 512, 1024], P('stage', 'data'), parts along dimension 0
- output 8: float32 [48, 512, 1024], P('stage', 'data'), parts along dimension 0
There are 4 independent parts. A program takes and returns all parts, laid end to end along the dimension named above; each array names one.
All inputs are finite; a program needn't handle non-finite values.
Results may differ from a plain program's by a relative error of at most 0.00416286.
Values are sent between devices in bfloat16 or wider.
A program may use at most 1 GiB of HBM per device.

v0:
```python
import math
import jax
import jax.numpy as jnp
from jax import lax
from jax.sharding import PartitionSpec as P

NS_STEPS = 5
COEF_A = 3.4445
COEF_B = -4.7750
COEF_C = 2.0315
MOMENTUM = 0.95
LEARN_RATE = 0.04
DECAY = 0.2
NORM_EPS = 1e-7
RMS_MATCH = 0.2


def newton_schulz(x_mat):
    row_count, col_count = x_mat.shape[1], x_mat.shape[2]
    for _ in range(NS_STEPS):
        if row_count > col_count:
            gram_mat = jnp.einsum("kmn,kmp->knp", x_mat, x_mat, preferred_element_type=jnp.float32).astype(jnp.bfloat16)
        else:
            gram_mat = jnp.einsum("kmn,kpn->kmp", x_mat, x_mat, preferred_element_type=jnp.float32).astype(jnp.bfloat16)
        gram_sq = jnp.einsum("kab,kbc->kac", gram_mat, gram_mat, preferred_element_type=jnp.float32)
        poly_mat = (COEF_B * gram_mat.astype(jnp.float32) + COEF_C * gram_sq).astype(jnp.bfloat16)
        if row_count > col_count:
            product = jnp.einsum("kmn,knp->kmp", x_mat, poly_mat, preferred_element_type=jnp.float32)
        else:
            product = jnp.einsum("kmp,kpn->kmn", poly_mat, x_mat, preferred_element_type=jnp.float32)
        x_mat = (COEF_A * x_mat.astype(jnp.float32) + product).astype(jnp.bfloat16)
    return x_mat


def keep_block(block):
    return block


def stack_update(weight, momentum, gradient, group_size):
    mat_count, local_rows, col_count = weight.shape
    row_count = local_rows * group_size
    new_mom = MOMENTUM * momentum + gradient.astype(jnp.float32)
    sq_sum = lax.psum(jnp.sum(new_mom * new_mom, axis=(1, 2)), "data")
    scaled = (new_mom / (jnp.sqrt(sq_sum)[:, None, None] + NORM_EPS)).astype(jnp.bfloat16)
    per_dev = -(-mat_count // group_size)
    padded = jnp.pad(scaled, ((0, per_dev * group_size - mat_count), (0, 0), (0, 0)))
    owned = lax.all_to_all(padded, "data", 0, 1, tiled=True)
    first_slot = lax.axis_index("data") * per_dev
    ortho_out = lax.cond(first_slot < mat_count, newton_schulz, keep_block, owned)
    returned = lax.all_to_all(ortho_out, "data", 1, 0, tiled=True)[:mat_count]
    rms_scale = RMS_MATCH * math.sqrt(max(row_count, col_count))
    new_weight = weight - LEARN_RATE * (rms_scale * returned.astype(jnp.float32) + DECAY * weight)
    return new_weight, new_mom


def solution(mesh):
    group_size = mesh.shape["data"]
    row_spec = P("stage", "data", None)

    def local_step(w_qkv, m_qkv, g_qkv, w_out, m_out, g_out, w_up, m_up, g_up, w_down, m_down, g_down):
        stacks = ((w_qkv, m_qkv, g_qkv), (w_out, m_out, g_out), (w_up, m_up, g_up), (w_down, m_down, g_down))
        results = []
        for weight, momentum, gradient in stacks:
            new_weight, new_mom = stack_update(weight, momentum, gradient, group_size)
            results.append(new_weight)
            results.append(new_mom)
        return tuple(results)

    return jax.shard_map(local_step, mesh=mesh, in_specs=(row_spec,) * 12, out_specs=(row_spec,) * 8, check_vma=False)
```

profile of v0, /device:TPU:9, one launch (start us, length us, event | category | flops | bytes accessed | tf_op | source)
XLA Modules:
  0.0 668.1 jit_solution(5855123516122094335)
XLA Ops:
  12.7 10.2 %all-reduce.4 = (f32[3]{0:T(128)S(1)}, f32[3]{0:T(128)S(1)}, f32[12]{0:T(128)S(1)}, f32[12]{0:T(128)S(1)}) all-reduce(f32[3]{0:T(128)S(1)} %get-tuple-element.38, f32[3]{0:T(128)S(1)} %get-tuple-element.36, f32[12]{0:T(128)S(1)} %get-tuple-element.34, f32[12]{0:T(128)S(1)} %get-tuple-element.32), channel_id=1, replica_groups=mesh['stage'=4,'data'=8] {'data'}, use_global_device_ids=true, to_apply=%region_1.0 | all-reduce | flops 30 | bytes 240 | tf_op jit(solution)/shard_map/psum | solution.py:43
  26.1 11.4 %all-to-all-start.2 = ((bf16[8,128,1024]{2,1,0:T(8,128)(2,1)}), bf16[8,128,1024]{2,1,0:T(8,128)(2,1)}, u32[]{:S(2)}, u32[]{:S(2)}) async-start(bf16[8,128,1024]{2,1,0:T(8,128)(2,1)} %pad.17), calls=%async_computation.2 | async-start | bytes 4194304 | tf_op jit(solution)/shard_map/all_to_all | solution.py:47
  41.4 41.4 %all-to-all-done.2 = bf16[8,128,1024]{2,1,0:T(8,128)(2,1)} async-done(((bf16[8,128,1024]{2,1,0:T(8,128)(2,1)}), bf16[8,128,1024]{2,1,0:T(8,128)(2,1)}, u32[]{:S(2)}, u32[]{:S(2)}) %all-to-all-start.2) | async-done | bytes 2097184 | tf_op jit(solution)/shard_map/all_to_all | solution.py:47
  82.8 7.9 %all-to-all-start.4 = ((bf16[16,128,512]{2,1,0:T(8,128)(2,1)}), bf16[16,128,512]{2,1,0:T(8,128)(2,1)}, u32[]{:S(2)}, u32[]{:S(2)}) async-start(bf16[16,128,512]{2,1,0:T(8,128)(2,1)} %pad.18), calls=%async_computation.4 | async-start | bytes 4194304 | tf_op jit(solution)/shard_map/all_to_all | solution.py:47
  92.7 43.2 %all-to-all-done.4 = bf16[16,128,512]{2,1,0:T(8,128)(2,1)} async-done(((bf16[16,128,512]{2,1,0:T(8,128)(2,1)}), bf16[16,128,512]{2,1,0:T(8,128)(2,1)}, u32[]{:S(2)}, u32[]{:S(2)}) %all-to-all-start.4) | async-done | bytes 2097184 | tf_op jit(solution)/shard_map/all_to_all | solution.py:47
  136.0 7.8 %all-to-all-start.6 = ((bf16[16,64,1024]{2,1,0:T(8,128)(2,1)}), bf16[16,64,1024]{2,1,0:T(8,128)(2,1)}, u32[]{:S(2)}, u32[]{:S(2)}) async-start(bf16[16,64,1024]{2,1,0:T(8,128)(2,1)} %pad.19), calls=%async_computation.6 | async-start | bytes 4194304 | tf_op jit(solution)/shard_map/all_to_all | solution.py:47
  146.6 42.5 %all-to-all-done.6 = bf16[16,64,1024]{2,1,0:T(8,128)(2,1)} async-done(((bf16[16,64,1024]{2,1,0:T(8,128)(2,1)}), bf16[16,64,1024]{2,1,0:T(8,128)(2,1)}, u32[]{:S(2)}, u32[]{:S(2)}) %all-to-all-start.6) | async-done | bytes 2097184 | tf_op jit(solution)/shard_map/all_to_all | solution.py:47
  189.1 8.1 %all-to-all-start = ((bf16[8,128,2048]{2,1,0:T(8,128)(2,1)}), bf16[8,128,2048]{2,1,0:T(8,128)(2,1)}, u32[]{:S(2)}, u32[]{:S(2)}) async-start(bf16[8,128,2048]{2,1,0:T(8,128)(2,1)} %pad.16), calls=%async_computation | async-start | bytes 8388608 | tf_op jit(solution)/shard_map/all_to_all | solution.py:47
  202.1 6.8 %copy.159 = bf16[1,1024,1024]{2,0,1:T(2,128)(2,1)} copy(bf16[1,1024,1024]{2,1,0:T(8,128)(2,1)} %get-tuple-element.45) | data formatting | bytes 4194304 | tf_op jit(solution)/shard_map/cond | solution.py:49
  209.5 12.8 %reduce.1 = bf16[1024,1024]{1,0:T(8,128)(2,1)S(1)} reduce(bf16[1024,1,1024]{2,1,0:T(2,128)(2,1)} %bitcast.221, bf16[]{:T(256)} %broadcast.232), dimensions={1}, to_apply=%bitcast.218.reduce_sub_computation | reduce | bytes 4194306
  226.0 61.4 %all-to-all-done = bf16[8,128,2048]{2,1,0:T(8,128)(2,1)} async-done(((bf16[8,128,2048]{2,1,0:T(8,128)(2,1)}), bf16[8,128,2048]{2,1,0:T(8,128)(2,1)}, u32[]{:S(2)}, u32[]{:S(2)}) %all-to-all-start) | async-done | bytes 4194336 | tf_op jit(solution)/shard_map/all_to_all | solution.py:47
  287.4 7.1 %all-to-all-start.3 = ((bf16[8,2,65536]{2,1,0:T(2,128)(2,1)}), bf16[8,2,65536]{2,1,0:T(2,128)(2,1)S(1)}, u32[]{:S(2)}, u32[]{:S(2)}) async-start(bf16[8,2,65536]{2,1,0:T(2,128)(2,1)} %reshape.252), calls=%async_computation.3 | async-start | bytes 4194304 | tf_op jit(solution)/shard_map/all_to_all | solution.py:50
  302.9 45.3 %conditional.6 = (bf16[2,1024,512]{1,2,0:T(8,128)(2,1)}) conditional(s32[]{:T(128)} %convert_element_type.393, bf16[2,1024,512]{1,2,0:T(8,128)(2,1)} %all_to_all.119, bf16[2,1024,512]{1,2,0:T(8,128)(2,1)} %all_to_all.119), branch_computations={%region_10.11_spmd, %region_11.12_spmd} | conditional | flops 13458472960 | bytes 41943048 | solution.py:49
  348.2 6.2 copy.124
  361.9 31.2 %conditional.7 = (bf16[2,512,1024]{2,1,0:T(8,128)(2,1)S(1)}) conditional(s32[]{:T(128)} %convert_element_type.393, bf16[2,512,1024]{2,1,0:T(8,128)(2,1)S(1)} %bitcast.223, bf16[2,512,1024]{2,1,0:T(8,128)(2,1)S(1)} %bitcast.224), branch_computations={%region_14.15_spmd, %region_15.16_spmd} | conditional | flops 13458472960 | bytes 50331684 | solution.py:49
  396.6 8.8 %all-to-all-done.5 = bf16[2,1024,512]{2,0,1:T(2,128)(2,1)} async-done(((bf16[2,1024,512]{2,0,1:T(2,128)(2,1)}), bf16[2,1024,512]{2,0,1:T(2,128)(2,1)}, u32[]{:S(2)}, u32[]{:S(2)}) %all-to-all-start.5) | async-done | bytes 2097184 | tf_op jit(solution)/shard_map/all_to_all | solution.py:50
  405.4 7.8 %all-to-all-start.7 = ((bf16[2,512,1024]{2,0,1:T(2,128)(2,1)}), bf16[2,512,1024]{2,0,1:T(2,128)(2,1)}, u32[]{:S(2)}, u32[]{:S(2)}) async-start(bf16[2,512,1024]{2,0,1:T(2,128)(2,1)} %copy.128), calls=%async_computation.7 | async-start | bytes 4194304 | tf_op jit(solution)/shard_map/all_to_all | solution.py:50
  416.7 8.6 %copy.158 = bf16[1,1024,2048]{2,0,1:T(2,128)(2,1)} copy(bf16[1,1024,2048]{2,1,0:T(8,128)(2,1)} %get-tuple-element.44) | data formatting | bytes 8388608 | tf_op jit(solution)/shard_map/cond | solution.py:49
  425.3 26.7 %reduce = bf16[1024,2048]{1,0:T(8,128)(2,1)} reduce(bf16[1024,1,2048]{2,1,0:T(2,128)(2,1)} %bitcast.219, bf16[]{:T(256)} %broadcast.232), dimensions={1}, to_apply=%bitcast.217.reduce_sub_computation | reduce | bytes 8388610
  452.0 7.8 %reshape.250 = bf16[8,2,131072]{2,1,0:T(2,128)(2,1)} reshape(bf16[1024,2048]{1,0:T(8,128)(2,1)} %reduce) | data formatting | bytes 8388608
  459.8 100.5 %all-to-all-start.1 = ((bf16[8,2,131072]{2,1,0:T(2,128)(2,1)}), bf16[8,2,131072]{2,1,0:T(2,128)(2,1)}, u32[]{:S(2)}, u32[]{:S(2)}) async-start(bf16[8,2,131072]{2,1,0:T(2,128)(2,1)} %reshape.250), calls=%async_computation.1 | async-start | bytes 8388608 | tf_op jit(solution)/shard_map/all_to_all | solution.py:50
  581.2 69.3 %all-to-all-done.1 = bf16[8,2,131072]{2,1,0:T(2,128)(2,1)} async-done(((bf16[8,2,131072]{2,1,0:T(2,128)(2,1)}), bf16[8,2,131072]{2,1,0:T(2,128)(2,1)}, u32[]{:S(2)}, u32[]{:S(2)}) %all-to-all-start.1) | async-done | bytes 4194336 | tf_op jit(solution)/shard_map/all_to_all | solution.py:50
  650.5 8.8 %reshape.251 = bf16[1024,1,2048]{2,1,0:T(2,128)(2,1)} reshape(bf16[8,2,131072]{2,1,0:T(2,128)(2,1)} %all-to-all-done.1) | data formatting | bytes 8388608
  659.4 6.2 copy.150
  (85 shorter events, 154.9 us)
Async XLA Ops:
  0.6 3.3 copy-start.4
  0.6 3.8 copy-start.11
  4.4 86.3 %copy-start = (f32[12,64,1024]{2,1,0:T(8,128)}, f32[12,64,1024]{2,1,0:T(8,128)S(1)}, u32[]{:S(2)}) copy-start(f32[12,64,1024]{2,1,0:T(8,128)S(1)} %get-tuple-element.33) | copy-start | bytes 9437188
  4.4 4.2 copy-start.5
  4.4 4.6 copy-start.12
  9.0 2.3 copy-start.9
  9.0 2.3 copy-start.13
  26.1 56.7 %all-to-all-start.2 = ((bf16[8,128,1024]{2,1,0:T(8,128)(2,1)}), bf16[8,128,1024]{2,1,0:T(8,128)(2,1)}, u32[]{:S(2)}, u32[]{:S(2)}) async-start(bf16[8,128,1024]{2,1,0:T(8,128)(2,1)} %pad.17), calls=%async_computation.2 | async-start | bytes 4194304 | tf_op jit(solution)/shard_map/all_to_all | solution.py:47
  82.8 53.1 %all-to-all-start.4 = ((bf16[16,128,512]{2,1,0:T(8,128)(2,1)}), bf16[16,128,512]{2,1,0:T(8,128)(2,1)}, u32[]{:S(2)}, u32[]{:S(2)}) async-start(bf16[16,128,512]{2,1,0:T(8,128)(2,1)} %pad.18), calls=%async_computation.4 | async-start | bytes 4194304 | tf_op jit(solution)/shard_map/all_to_all | solution.py:47
  92.7 51.1 %copy-start.1 = (f32[3,128,2048]{2,1,0:T(8,128)S(1)}, f32[3,128,2048]{2,1,0:T(8,128)}, u32[]{:S(2)}) copy-start(f32[3,128,2048]{2,1,0:T(8,128)} %get-tuple-element.39) | copy-start | bytes 9437188
  136.0 53.1 %all-to-all-start.6 = ((bf16[16,64,1024]{2,1,0:T(8,128)(2,1)}), bf16[16,64,1024]{2,1,0:T(8,128)(2,1)}, u32[]{:S(2)}, u32[]{:S(2)}) async-start(bf16[16,64,1024]{2,1,0:T(8,128)(2,1)} %pad.19), calls=%async_computation.6 | async-start | bytes 4194304 | tf_op jit(solution)/shard_map/all_to_all | solution.py:47
  189.1 98.3 %all-to-all-start = ((bf16[8,128,2048]{2,1,0:T(8,128)(2,1)}), bf16[8,128,2048]{2,1,0:T(8,128)(2,1)}, u32[]{:S(2)}, u32[]{:S(2)}) async-start(bf16[8,128,2048]{2,1,0:T(8,128)(2,1)} %pad.16), calls=%async_computation | async-start | bytes 8388608 | tf_op jit(solution)/shard_map/all_to_all | solution.py:47
  287.4 67.0 %all-to-all-start.3 = ((bf16[8,2,65536]{2,1,0:T(2,128)(2,1)}), bf16[8,2,65536]{2,1,0:T(2,128)(2,1)S(1)}, u32[]{:S(2)}, u32[]{:S(2)}) async-start(bf16[8,2,65536]{2,1,0:T(2,128)(2,1)} %reshape.252), calls=%async_computation.3 | async-start | bytes 4194304 | tf_op jit(solution)/shard_map/all_to_all | solution.py:50
  354.4 1.3 copy-start.2
  355.7 49.7 %all-to-all-start.5 = ((bf16[2,1024,512]{2,0,1:T(2,128)(2,1)}), bf16[2,1024,512]{2,0,1:T(2,128)(2,1)}, u32[]{:S(2)}, u32[]{:S(2)}) async-start(bf16[2,1024,512]{2,0,1:T(2,128)(2,1)} %copy.124), calls=%async_computation.5 | async-start | bytes 4194304 | tf_op jit(solution)/shard_map/all_to_all | solution.py:50
  386.2 1.3 copy-start.14
  405.4 54.5 %all-to-all-start.7 = ((bf16[2,512,1024]{2,0,1:T(2,128)(2,1)}), bf16[2,512,1024]{2,0,1:T(2,128)(2,1)}, u32[]{:S(2)}, u32[]{:S(2)}) async-start(bf16[2,512,1024]{2,0,1:T(2,128)(2,1)} %copy.128), calls=%async_computation.7 | async-start | bytes 4194304 | tf_op jit(solution)/shard_map/all_to_all | solution.py:50
  459.8 100.5 %copy-start.3 = (bf16[8,2,65536]{2,1,0:T(2,128)(2,1)S(1)}, bf16[8,2,65536]{2,1,0:T(2,128)(2,1)}, u32[]{:S(2)}) copy-start(bf16[8,2,65536]{2,1,0:T(2,128)(2,1)} %copy-done.2) | copy-start | bytes 6291460
  459.8 190.7 %all-to-all-start.1 = ((bf16[8,2,131072]{2,1,0:T(2,128)(2,1)}), bf16[8,2,131072]{2,1,0:T(2,128)(2,1)}, u32[]{:S(2)}, u32[]{:S(2)}) async-start(bf16[8,2,131072]{2,1,0:T(2,128)(2,1)} %reshape.250), calls=%async_computation.1 | async-start | bytes 8388608 | tf_op jit(solution)/shard_map/all_to_all | solution.py:50
  569.8 2.4 copy-start.10
  574.1 1.9 copy-start.6
  576.0 2.5 copy-start.7
  659.4 6.2 copy-start.8
where the time goes:
time: 678 us; the launch traced here: 668 us
  waiting for transfers between devices  267 us (39%)
  starting transfers between devices  155 us (23%)
  local copies, waits for them, and re-layouts  88.6 us (13%)
  matrix products  74.3 us (11%)
  other arithmetic  63.2 us (9%)
  blocking collectives  10.2 us (2%)
  loops' own time  9.27 us (1%)
    all_to_all x4, waiting for transfers between devices, stack_update(): owned = lax.all_to_all(padded, 'data', 0, 1, tiled=True)  188 us
    all_to_all x4, starting transfers between devices, stack_update(): returned = lax.all_to_all(ortho_out, 'data', 1, 0, tiled=True)[:mat_count]  120 us
    all_to_all x4, waiting for transfers between devices, stack_update(): returned = lax.all_to_all(ortho_out, 'data', 1, 0, tiled=True)[:mat_count]  78.1 us
    unnamed x35, local copies, waits for them, and re-layouts  40.4 us
    unnamed x2, other arithmetic  39.4 us
    all_to_all x4, starting transfers between devices, stack_update(): owned = lax.all_to_all(padded, 'data', 0, 1, tiled=True)  35.2 us
    dot_general x5, matrix products, newton_schulz(): jnp.einsum('kmn,knp->kmp', x_mat, poly_mat, preferred_element_type=jnp.fl...  27.2 us
    cond x4, local copies, waits for them, and re-layouts, stack_update(): lax.cond(first_slot < mat_count, newton_schulz, keep_block, owned)  25.1 us
  transfers between devices with their start and end apart: 8, of which 6 were waited for; matrix products, arithmetic and copies ran while one was open for 28% of the time, Pallas kernels for 0%

commit v1 on v0

v1 whole, which is shorter than its diff:
```python
import functools
import math
import jax
import jax.numpy as jnp
from jax import lax
from jax.experimental import pallas as pl
from jax.experimental.pallas import tpu as pltpu
from jax.sharding import PartitionSpec as P

NS_STEPS = 5
COEF_A = 3.4445
COEF_B = -4.7750
COEF_C = 2.0315
MOMENTUM = 0.95
LEARN_RATE = 0.04
DECAY = 0.2
NORM_EPS = 1e-7
RMS_MATCH = 0.2

GROUP = 8
MESH = pl.DeviceIdType.MESH
NT = (((1,), (1,)), ((), ()))
F32 = jnp.float32
BF16 = jnp.bfloat16

QKV_OWNER = (0, 1, 7)
OUT_OWNER = (2, 4, 6)
EXPERT_COUNT = (0, 0, 3, 8, 3, 7, 3, 0)
EXPERT_BASE = (0, 0, 0, 3, 11, 14, 21, 24)
EXPERT_OWNER = tuple(d for d in range(GROUP) for _ in range(EXPERT_COUNT[d]))
N_DOWN = 12
MAX_EXPERTS = 8


def send_order():
    halves = ([], [])
    sizes = {"q": 4, "o": 2, "e": 1}
    for kind, owners in (("q", QKV_OWNER), ("o", OUT_OWNER)):
        for index, owner in enumerate(owners):
            halves[owner // 4].append((kind, index))
    for half in range(2):
        devices = [d for d in range(4 * half, 4 * half + 4) if EXPERT_COUNT[d]]
        slots = []
        for d in devices:
            for t in range(EXPERT_COUNT[d]):
                slots.append(((t + 0.5) / EXPERT_COUNT[d], d, t))
        for _, d, t in sorted(slots):
            halves[half].append(("e", EXPERT_BASE[d] + t))
    order, sent, place = [], [0, 0], [0, 0]
    while place[0] < len(halves[0]) or place[1] < len(halves[1]):
        half = 0 if sent[0] <= sent[1] else 1
        if place[half] == len(halves[half]):
            half = 1 - half
        item = halves[half][place[half]]
        place[half] += 1
        sent[half] += sizes[item[0]]
        order.append(item)
    return order


ORDER = send_order()


def pick(table, me):
    total = jnp.int32(0)
    for d, value in enumerate(table):
        if value:
            total = total + jnp.where(me == d, jnp.int32(value), jnp.int32(0))
    return total


def ns_step(src, dst, gram, poly, m, block):
    def rows_of(i):
        return pl.ds(pl.multiple_of(i * block, block), block)

    @pl.loop(0, m // block)
    def _(i):
        rows = rows_of(i)
        gram[rows, :] = lax.dot_general(src[rows, :], src[...], NT, preferred_element_type=F32).astype(BF16)

    @pl.loop(0, m // block)
    def _(i):
        rows = rows_of(i)
        part = gram[rows, :]
        square = jnp.dot(part, gram[...], preferred_element_type=F32)
        poly[rows, :] = (COEF_B * part.astype(F32) + COEF_C * square).astype(BF16)

    @pl.loop(0, m // block)
    def _(i):
        rows = rows_of(i)
        product = jnp.dot(poly[rows, :], src[...], preferred_element_type=F32)
        dst[rows, :] = (COEF_A * src[rows, :].astype(F32) + product).astype(BF16)


def kernel(xq, xo, xd, xu, rq, ro, rd, ru, qbuf, obuf, ebuf, gram, poly, gram_e, poly_e,
           fwd_send, fwd_recv, ret_send, ret_recv):
    me = lax.axis_index("data")
    barrier = pltpu.get_barrier_semaphore()
    for k in range(1, GROUP):
        pl.semaphore_signal(barrier, inc=1, device_id={"data": lax.rem(me + k, GROUP)}, device_id_type=MESH)
    pl.semaphore_wait(barrier, GROUP - 1)

    def block_of(kind, index, slot_ref, d):
        if kind == "q" or kind == "o":
            return slot_ref.at[pl.ds(d * 128, 128), :]
        if kind == "d":
            return slot_ref.at[pl.ds(d * 64, 64), :]
        return slot_ref.at[:, pl.ds(d * 128, 128)]

    for number, (kind, index) in enumerate(ORDER):
        if kind == "q":
            owner, src, slot, sub, sem = QKV_OWNER[index], xq.at[index], qbuf.at[0], "q", index
        elif kind == "o":
            owner, src, slot, sub, sem = OUT_OWNER[index], xo.at[index], obuf.at[0], "o", 3 + index
        else:
            owner = EXPERT_OWNER[index]
            slot, sem = ebuf.at[index - EXPERT_BASE[owner]], 6 + index
            sub, src = ("d", xd.at[index]) if index < N_DOWN else ("u", xu.at[index - N_DOWN])

        @pl.when(me != owner)
        def _():
            pltpu.make_async_remote_copy(
                src_ref=src, dst_ref=block_of(sub, index, slot, me), send_sem=fwd_send.at[sem], recv_sem=fwd_recv.at[sem],
                device_id={"data": owner}, device_id_type=MESH).start()

        @pl.when(me == owner)
        def _():
            pltpu.make_async_copy(src, block_of(sub, index, slot, me), fwd_recv.at[sem]).start()

    def wait_whole(slot, sem):
        pltpu.make_async_copy(slot, slot, sem).wait()

    def give_back(kind, slot, out, send_sem, recv_sem):
        for k in range(1, GROUP):
            dst = lax.rem(me + k, GROUP)
            pltpu.make_async_remote_copy(
                src_ref=block_of(kind, 0, slot, dst), dst_ref=out, send_sem=send_sem, recv_sem=recv_sem,
                device_id={"data": dst}, device_id_type=MESH).start()
        pltpu.make_async_copy(block_of(kind, 0, slot, me), out, recv_sem).start()

    def wait_given(kind, slot, send_sem):
        rows = {"q": 896, "o": 896, "d": 448}
        part = slot.at[:, pl.ds(0, 896)] if kind == "u" else slot.at[pl.ds(0, rows[kind]), :]
        pltpu.make_async_copy(part, part, send_sem).wait()

    for index, owner in enumerate(QKV_OWNER):
        @pl.when(me == owner)
        def _():
            wait_whole(qbuf.at[0], fwd_recv.at[index])

    @pl.when((me == QKV_OWNER[0]) | (me == QKV_OWNER[1]) | (me == QKV_OWNER[2]))
    def _():
        @pl.loop(0, NS_STEPS)
        def _(it):
            now = lax.rem(it, 2)
            ns_step(qbuf.at[now], qbuf.at[1 - now], gram, poly, 1024, 256)

    for index, owner in enumerate(QKV_OWNER):
        @pl.when(me == owner)
        def _():
            give_back("q", qbuf.at[1], rq.at[index], ret_send.at[0], ret_recv.at[index])

    for index, owner in enumerate(OUT_OWNER):
        @pl.when(me == owner)
        def _():
            wait_whole(obuf.at[0], fwd_recv.at[3 + index])

    @pl.when((me == OUT_OWNER[0]) | (me == OUT_OWNER[1]) | (me == OUT_OWNER[2]))
    def _():
        @pl.loop(0, NS_STEPS)
        def _(it):
            now = lax.rem(it, 2)
            ns_step(obuf.at[now], obuf.at[1 - now], gram, poly, 1024, 256)

    for index, owner in enumerate(OUT_OWNER):
        @pl.when(me == owner)
        def _():
            give_back("o", obuf.at[1], ro.at[index], ret_send.at[1], ret_recv.at[3 + index])

    base, count = pick(EXPERT_BASE, me), pick(EXPERT_COUNT, me)

    @pl.loop(0, count)
    def _(t):
        rank = base + t
        wait_whole(ebuf.at[t], fwd_recv.at[6 + rank])

        @pl.loop(0, NS_STEPS)
        def _(it):
            src = jnp.where(it == 0, t, MAX_EXPERTS + lax.rem(it + 1, 2))
            dst = jnp.where(it == NS_STEPS - 1, t, MAX_EXPERTS + lax.rem(it, 2))
            ns_step(ebuf.at[src], ebuf.at[dst], gram_e, poly_e, 512, 256)

        @pl.when(rank < N_DOWN)
        def _():
            give_back("d", ebuf.at[t], rd.at[rank], ret_send.at[2 + t], ret_recv.at[6 + rank])

        @pl.when(rank >= N_DOWN)
        def _():
            give_back("u", ebuf.at[t], ru.at[rank - N_DOWN], ret_send.at[2 + t], ret_recv.at[6 + rank])

    for number, (kind, index) in enumerate(ORDER):
        if kind == "q":
            owner, src, out, sem = QKV_OWNER[index], xq.at[index], rq.at[index], index
        elif kind == "o":
            owner, src, out, sem = OUT_OWNER[index], xo.at[index], ro.at[index], 3 + index
        else:
            owner, sem = EXPERT_OWNER[index], 6 + index
            if index < N_DOWN:
                src, out = xd.at[index], rd.at[index]
            else:
                src, out = xu.at[index - N_DOWN], ru.at[index - N_DOWN]

        @pl.when(me != owner)
        def _():
            pltpu.make_async_copy(src, src, fwd_send.at[sem]).wait()

        pltpu.make_async_copy(out, out, ret_recv.at[sem]).wait()

    for owner in QKV_OWNER:
        @pl.when(me == owner)
        def _():
            wait_given("q", qbuf.at[1], ret_send.at[0])
    for owner in OUT_OWNER:
        @pl.when(me == owner)
        def _():
            wait_given("o", obuf.at[1], ret_send.at[1])

    @pl.loop(0, count)
    def _(t):
        @pl.when(base + t < N_DOWN)
        def _():
            wait_given("d", ebuf.at[t], ret_send.at[2 + t])

        @pl.when(base + t >= N_DOWN)
        def _():
            wait_given("u", ebuf.at[t], ret_send.at[2 + t])


def exchange(xq, xo, xd, xu):
    any_space = pl.BlockSpec(memory_space=pl.ANY)
    return pl.pallas_call(
        kernel,
        out_shape=[jax.ShapeDtypeStruct(x.shape, BF16) for x in (xq, xo, xd, xu)],
        in_specs=[any_space] * 4,
        out_specs=[any_space] * 4,
        scratch_shapes=[
            pltpu.VMEM((2, 1024, 2048), BF16),
            pltpu.VMEM((2, 1024, 1024), BF16),
            pltpu.VMEM((MAX_EXPERTS + 2, 512, 1024), BF16),
            pltpu.VMEM((1024, 1024), BF16),
            pltpu.VMEM((1024, 1024), BF16),
            pltpu.VMEM((512, 512), BF16),
            pltpu.VMEM((512, 512), BF16),
            pltpu.SemaphoreType.DMA((30,)),
            pltpu.SemaphoreType.DMA((30,)),
            pltpu.SemaphoreType.DMA((2 + MAX_EXPERTS,)),
            pltpu.SemaphoreType.DMA((30,)),
        ],
        compiler_params=pltpu.CompilerParams(
            collective_id=0, has_side_effects=True, vmem_limit_bytes=58 * 1024 * 1024),
    )(xq, xo, xd, xu)


def solution(mesh):
    row_spec = P("stage", "data", None)

    def local_step(w_qkv, m_qkv, g_qkv, w_out, m_out, g_out, w_up, m_up, g_up, w_down, m_down, g_down):
        moms, sums = [], []
        for momentum, gradient in ((m_qkv, g_qkv), (m_out, g_out), (m_up, g_up), (m_down, g_down)):
            new_mom = MOMENTUM * momentum + gradient.astype(F32)
            moms.append(new_mom)
            sums.append(jnp.sum(new_mom * new_mom, axis=(1, 2)))
        sums = lax.psum(tuple(sums), "data")
        scaled = [(m / (jnp.sqrt(s)[:, None, None] + NORM_EPS)).astype(BF16) for m, s in zip(moms, sums)]
        xq, xo, xu, xd = scaled
        rq, ro, rd, ru = exchange(xq, xo, xd, xu.transpose(0, 2, 1))
        results = []
        for weight, new_mom, back in ((w_qkv, moms[0], rq), (w_out, moms[1], ro), (w_up, moms[2], ru.transpose(0, 2, 1)),
                                      (w_down, moms[3], rd)):
            rms_scale = RMS_MATCH * math.sqrt(max(weight.shape[1] * GROUP, weight.shape[2]))
            results.append(weight - LEARN_RATE * (rms_scale * back.astype(F32) + DECAY * weight))
            results.append(new_mom)
        return tuple(results)

    return jax.shard_map(local_step, mesh=mesh, in_specs=(row_spec,) * 12, out_specs=(row_spec,) * 8, check_vma=False)
```

time: 678 us -> 309 us (0.46); the launches traced: 668 us -> 308 us
  waiting for transfers between devices: 267 us -> 0 us
  Pallas kernels: 0 us -> 246 us
  starting transfers between devices: 155 us -> 0 us
  matrix products: 74.3 us -> 0 us
  local copies, waits for them, and re-layouts: 88.6 us -> 15.6 us
  other arithmetic: 63.2 us -> 35.1 us
  loops' own time: 9.27 us -> 0 us
    all_to_all x8 -> x0, waiting for transfers between devices: 267 us -> none  [the longest x4 188 us: stack_update(): owned = lax.all_to_all(padded, 'data', 0, 1, tiled=True)]
    pallas_call x0 -> x1, Pallas kernels: none -> 246 us  [exchange(): pl.pallas_call(kernel, out_shape=[jax.ShapeDtypeStruct(x.shape, BF16) for...]
    all_to_all x8 -> x0, starting transfers between devices: 155 us -> none  [the longest x4 120 us: stack_update(): returned = lax.all_to_all(ortho_out, 'data', 1, 0, tiled=True)[:mat_count]]
    dot_general x20 -> x0, matrix products: 74.3 us -> none  [the longest x5 27.2 us: newton_schulz(): jnp.einsum('kmn,knp->kmp', x_mat, poly_mat, preferred_element_type=jnp.fl...]
    unnamed x2 -> x0, other arithmetic: 39.4 us -> none
    cond x6 -> x0, local copies, waits for them, and re-layouts: 26.4 us -> none  [the longest x4 25.1 us: stack_update(): lax.cond(first_slot < mat_count, newton_schulz, keep_block, owned)]
    unnamed x35 -> x23, local copies, waits for them, and re-layouts: 40.4 us -> 15.6 us
    all_to_all x5 -> x0, local copies, waits for them, and re-layouts: 14.7 us -> none  [the longest x3 10.3 us: stack_update(): owned = lax.all_to_all(padded, 'data', 0, 1, tiled=True)]
  transfers between devices with their start and end apart: 8 -> 0, of which waited for: 6 -> 0; matrix products, arithmetic and copies ran while one was open for 28% -> 0% of each run, Pallas kernels for 0% -> 0%
where the time goes in v1:
time: 309 us; the launch traced here: 308 us
  Pallas kernels  246 us (80%)
  other arithmetic  35.1 us (11%)
  local copies, waits for them, and re-layouts  15.6 us (5%)
  blocking collectives  10.2 us (3%)
    pallas_call x1, Pallas kernels, exchange(): pl.pallas_call(kernel, out_shape=[jax.ShapeDtypeStruct(x.shape, BF16) for...  246 us
    sub x4, other arithmetic, local_step(): weight - LEARN_RATE * (rms_scale * back.astype(F32) + DECAY * weight)  15.8 us
    unnamed x23, local copies, waits for them, and re-layouts  15.6 us
    reduce_sum x4, other arithmetic, local_step(): sums.append(jnp.sum(new_mom * new_mom, axis=(1, 2)))  11.4 us
    psum x1, blocking collectives, local_step(): sums = lax.psum(tuple(sums), 'data')  10.2 us
    convert_element_type x3, other arithmetic, local_step(): (m / (jnp.sqrt(s)[:, None, None] + NORM_EPS)).astype(BF16)  6.32 us

profile of v1, /device:TPU:9, one launch (start us, length us, event | category | flops | bytes accessed | tf_op | source)
XLA Modules:
  0.0 307.9 jit_solution(9210830528610514133)
XLA Ops:
  0.7 4.8 %multiply_reduce_fusion.2 = (f32[3]{0:T(128)S(1)}, f32[3,128,2048]{2,1,0:T(8,128)}) fusion(bf16[3,128,2048]{2,1,0:T(8,128)(2,1)} %param.14, f32[3,128,2048]{2,1,0:T(8,128)} %param.13), kind=kLoop, calls=%fused_computation.12 | loop fusion | flops 3932157 | bytes 7864332 | tf_op jit(solution)/shard_map/reduce_sum | solution.py:272
  5.4 1.4 multiply_reduce_fusion.3
  6.9 0.0 copy-done.6
  6.9 1.0 copy-done.3
  7.9 2.2 multiply_reduce_fusion.1
  10.1 2.7 copy.21
  12.8 2.4 copy.20
  15.2 3.0 multiply_reduce_fusion
  18.2 10.2 %all-reduce = (f32[3]{0:T(128)S(1)}, f32[3]{0:T(128)S(1)}, f32[12]{0:T(128)S(1)}, f32[12]{0:T(128)S(1)}) all-reduce(f32[3]{0:T(128)S(1)} %get-tuple-element.34, f32[3]{0:T(128)S(1)} %get-tuple-element.32, f32[12]{0:T(128)S(1)} %get-tuple-element.30, f32[12]{0:T(128)S(1)} %get-tuple-element.28), channel_id=1, replica_groups=mesh['stage'=4,'data'=8] {'data'}, use_global_device_ids=true, to_apply=%region_1.0 | all-reduce | flops 30 | bytes 240 | tf_op jit(solution)/shard_map/psum | solution.py:273
  28.4 0.0 copy-start
  28.4 3.6 %divide_convert_fusion.2.xq = bf16[3,128,2048]{2,1,0:T(8,128)(2,1)} fusion(f32[3,128,2048]{2,1,0:T(8,128)} %get-tuple-element.35, f32[3]{0:T(128)S(1)} %get-tuple-element.39), kind=kLoop, calls=%fused_computation.11 | loop fusion | flops 1572864 | bytes 4718604 | tf_op jit(solution)/shard_map/convert_element_type | solution.py:274
  32.0 1.1 divide_convert_fusion.3.xo
  33.1 1.7 divide_convert_fusion.1.xd
  34.7 1.6 fusion.2.xu
  36.3 246.3 %shard_map.179 = (bf16[3,128,2048]{2,1,0:T(8,128)(2,1)}, bf16[3,128,1024]{2,1,0:T(8,128)(2,1)}, bf16[12,64,1024]{2,1,0:T(8,128)(2,1)}, bf16[12,512,128]{2,1,0:T(8,128)(2,1)}) custom-call(bf16[3,128,2048]{2,1,0:T(8,128)(2,1)} %divide_convert_fusion.2.xq, bf16[3,128,1024]{2,1,0:T(8,128)(2,1)} %divide_convert_fusion.3.xo, ...), custom_call_target="tpu_custom_call" | custom-call | tf_op jit(solution)/shard_map/pallas_call | solution.py:241
  282.6 0.0 copy-start.5
  282.6 4.9 %multiply_subtract_fusion.1 = f32[3,128,2048]{2,1,0:T(8,128)} fusion(f32[3,128,2048]{2,1,0:T(8,128)} %param.12, bf16[3,128,2048]{2,1,0:T(8,128)(2,1)} %get-tuple-element.12), kind=kLoop, calls=%fused_computation.4 | loop fusion | flops 4718592 | bytes 7864320 | tf_op jit(solution)/shard_map/sub | solution.py:281
  287.5 0.0 copy-done.5
  287.5 1.5 multiply_subtract_fusion.2
  289.0 3.5 %copy.23 = f32[12,128,512]{1,2,0:T(8,128)} copy(f32[12,128,512]{2,1,0:T(8,128)} %param.18) | data formatting | bytes 6291456 | tf_op args[6]
  292.5 4.6 %fusion.1 = f32[12,128,512]{1,2,0:T(8,128)} fusion(f32[12,128,512]{1,2,0:T(8,128)} %copy.23, bf16[12,512,128]{2,1,0:T(8,128)(2,1)} %get-tuple-element.14), kind=kLoop, calls=%fused_computation.2 | loop fusion | flops 4718592 | bytes 7864320 | tf_op jit(solution)/shard_map/sub | solution.py:281
  297.2 3.5 %copy.24 = f32[12,128,512]{2,1,0:T(8,128)} copy(f32[12,128,512]{1,2,0:T(8,128)} %fusion.1) | data formatting | bytes 6291456
  300.7 2.4 copy.25
  303.1 4.8 %multiply_subtract_fusion = f32[12,64,1024]{2,1,0:T(8,128)} fusion(f32[12,64,1024]{2,1,0:T(8,128)} %param.21, bf16[12,64,1024]{2,1,0:T(8,128)(2,1)} %get-tuple-element.15), kind=kLoop, calls=%fused_computation.3 | loop fusion | flops 4718592 | bytes 7864320 | tf_op jit(solution)/shard_map/sub | solution.py:281
  (15 shorter events, 0.0 us)
Async XLA Ops:
  0.6 4.8 %copy-start.7 = (bf16[3,128,1024]{2,1,0:T(8,128)(2,1)S(1)}, bf16[3,128,1024]{2,1,0:T(8,128)(2,1)}, u32[]{:S(2)}) copy-start(bf16[3,128,1024]{2,1,0:T(8,128)(2,1)} %param.17) | copy-start | bytes 2359300
  0.6 4.8 %copy-start.4 = (f32[3,128,1024]{2,1,0:T(8,128)S(1)}, f32[3,128,1024]{2,1,0:T(8,128)}, u32[]{:S(2)}) copy-start(f32[3,128,1024]{2,1,0:T(8,128)} %param.16) | copy-start | bytes 4718596
  0.7 6.2 %copy-start.6 = (bf16[12,64,1024]{2,1,0:T(8,128)(2,1)S(1)}, bf16[12,64,1024]{2,1,0:T(8,128)(2,1)}, u32[]{:S(2)}) copy-start(bf16[12,64,1024]{2,1,0:T(8,128)(2,1)} %param.23) | copy-start | bytes 4718596
  5.4 2.5 copy-start.3
  10.1 2.7 copy-start.2
  28.4 3.6 %copy-start.1 = (f32[3,128,1024]{2,1,0:T(8,128)S(1)}, f32[3,128,1024]{2,1,0:T(8,128)}, u32[]{:S(2)}) copy-start(f32[3,128,1024]{2,1,0:T(8,128)} %get-tuple-element.33) | copy-start | bytes 4718596
  28.4 4.7 %copy-start = (f32[12,64,1024]{2,1,0:T(8,128)S(1)}, f32[12,64,1024]{2,1,0:T(8,128)}, u32[]{:S(2)}) copy-start(f32[12,64,1024]{2,1,0:T(8,128)} %get-tuple-element.31) | copy-start | bytes 9437188
  282.6 4.9 %copy-start.5 = (f32[3,128,1024]{2,1,0:T(8,128)S(1)}, f32[3,128,1024]{2,1,0:T(8,128)}, u32[]{:S(2)}) copy-start(f32[3,128,1024]{2,1,0:T(8,128)} %param.15) | copy-start | bytes 4718596
  282.6 4.9 %copy-start.8 = (bf16[3,128,1024]{2,1,0:T(8,128)(2,1)S(1)}, bf16[3,128,1024]{2,1,0:T(8,128)(2,1)}, u32[]{:S(2)}) copy-start(bf16[3,128,1024]{2,1,0:T(8,128)(2,1)} %get-tuple-element.13) | copy-start | bytes 2359300

commit v2 on v1

v2 whole, which is shorter than its diff:
```python
import math
import jax
import jax.numpy as jnp
from jax import lax
from jax.experimental import pallas as pl
from jax.experimental.pallas import tpu as pltpu
from jax.sharding import PartitionSpec as P

NS_STEPS = 5
COEF_A = 3.4445
COEF_B = -4.7750
COEF_C = 2.0315
MOMENTUM = 0.95
LEARN_RATE = 0.04
DECAY = 0.2
NORM_EPS = 1e-7
RMS_MATCH = 0.2

GROUP = 8
MESH = pl.DeviceIdType.MESH
NT = (((1,), (1,)), ((), ()))
F32 = jnp.float32
BF16 = jnp.bfloat16

QKV_OWNER = (0, 1, 7)
OUT_OWNER = (2, 4, 6)
EXPERT_COUNT = (0, 0, 3, 8, 3, 7, 3, 0)
EXPERT_BASE = (0, 0, 0, 3, 11, 14, 21, 24)
EXPERT_OWNER = tuple(d for d in range(GROUP) for _ in range(EXPERT_COUNT[d]))
N_DOWN = 12
MAX_EXPERTS = 8
VMEM_LIMIT = 40 * 1024 * 1024


def send_order():
    halves = ([], [])
    sizes = {"q": 4, "o": 2, "e": 1}
    for kind, owners in (("q", QKV_OWNER), ("o", OUT_OWNER)):
        for index, owner in enumerate(owners):
            halves[owner // 4].append((kind, index))
    for half in range(2):
        devices = [d for d in range(4 * half, 4 * half + 4) if EXPERT_COUNT[d]]
        slots = []
        for d in devices:
            for t in range(EXPERT_COUNT[d]):
                slots.append(((t + 0.5) / EXPERT_COUNT[d], d, t))
        for _, d, t in sorted(slots):
            halves[half].append(("e", EXPERT_BASE[d] + t))
    order, sent, place = [], [0, 0], [0, 0]
    while place[0] < len(halves[0]) or place[1] < len(halves[1]):
        half = 0 if sent[0] <= sent[1] else 1
        if place[half] == len(halves[half]):
            half = 1 - half
        item = halves[half][place[half]]
        place[half] += 1
        sent[half] += sizes[item[0]]
        order.append(item)
    return order


ORDER = send_order()


def pick(table, me):
    total = jnp.int32(0)
    for d, value in enumerate(table):
        if value:
            total = total + jnp.where(me == d, jnp.int32(value), jnp.int32(0))
    return total


def ns_step(src, dst, gram, poly, m, block):
    def rows_of(i):
        return pl.ds(pl.multiple_of(i * block, block), block)

    @pl.loop(0, m // block)
    def _(i):
        rows = rows_of(i)
        gram[rows, :] = lax.dot_general(src[rows, :], src[...], NT, preferred_element_type=F32).astype(BF16)

    @pl.loop(0, m // block)
    def _(i):
        rows = rows_of(i)
        part = gram[rows, :]
        square = jnp.dot(part, gram[...], preferred_element_type=F32)
        poly[rows, :] = (COEF_B * part.astype(F32) + COEF_C * square).astype(BF16)

    @pl.loop(0, m // block)
    def _(i):
        rows = rows_of(i)
        product = jnp.dot(poly[rows, :], src[...], preferred_element_type=F32)
        dst[rows, :] = (COEF_A * src[rows, :].astype(F32) + product).astype(BF16)


STACKS = {"q": (3, 128, 2048, 32, 0), "o": (3, 128, 1024, 64, 0), "d": (12, 64, 1024, 64, 3), "u": (12, 128, 512, 128, 15)}
SCALE = {"q": RMS_MATCH * math.sqrt(2048), "o": RMS_MATCH * math.sqrt(1024),
         "d": RMS_MATCH * math.sqrt(1024), "u": RMS_MATCH * math.sqrt(1024)}
SEM_BASE = {"q": 0, "o": 3, "d": 6, "u": 18}


def place_of(kind, index):
    if kind == "q":
        return "q", index, QKV_OWNER[index], 0
    if kind == "o":
        return "o", index, OUT_OWNER[index], 0
    owner = EXPERT_OWNER[index]
    slot = index - EXPERT_BASE[owner]
    return ("d", index, owner, slot) if index < N_DOWN else ("u", index - N_DOWN, owner, slot)


def return_order():
    keys = []
    for kind, index in ORDER:
        stack, position, owner, slot = place_of(kind, index)
        total = 4 if kind == "q" else EXPERT_COUNT[owner] + (2 if owner in OUT_OWNER else 0)
        if kind == "q":
            done = 0.6 * total
        else:
            done = 2 if kind == "o" else slot + 1 + (2 if owner in OUT_OWNER else 0)
        keys.append((done / total, len(keys), stack, position))
    return [(stack, position) for _, _, stack, position in sorted(keys)]


RETURNS = return_order()


def kernel(w_q, m_q, g_q, w_o, m_o, g_o, w_u, m_u, g_u, w_d, m_d, g_d,
           nw_q, nm_q, nw_o, nm_o, nw_u, nm_u, nw_d, nm_d,
           big, ebuf, gram, poly, xs_q, xs_o, xs_d, xs_u, bk_q, bk_o, bk_d, gs_u, bk_u,
           part_q, part_e, gath_q, gath_e, den_q, den_e,
           m_sem, g_sem, w_sem, norm_send, norm_recv, fwd_send, fwd_recv, ret_send, ret_recv):
    me = lax.axis_index("data")
    weights = {"q": w_q, "o": w_o, "d": w_d, "u": w_u}
    momenta = {"q": m_q, "o": m_o, "d": m_d, "u": m_u}
    gradients = {"q": g_q, "o": g_o, "d": g_d, "u": g_u}
    new_w = {"q": nw_q, "o": nw_o, "d": nw_d, "u": nw_u}
    new_m = {"q": nm_q, "o": nm_o, "d": nm_d, "u": nm_u}
    grad_in = {"q": bk_q, "o": bk_o, "d": bk_d, "u": gs_u}
    scaled = {"q": xs_q, "o": xs_o, "d": xs_d, "u": xs_u}
    back = {"q": bk_q, "o": bk_o, "d": bk_d, "u": bk_u}

    loads = {"q": [("q", i) for i in range(3)], "o": [("o", None)], "d": [("d", None)], "u": [("u", None)]}
    load_sem = {("q", 0): 0, ("q", 1): 1, ("q", 2): 2, ("o", None): 3, ("d", None): 4, ("u", None): 5}

    def part_of(ref, i):
        return ref if i is None else ref.at[i]

    def load_copies(key):
        stack, i = key
        sem = load_sem[key]
        return (pltpu.make_async_copy(part_of(momenta[stack], i), part_of(new_m[stack], i), m_sem.at[sem]),
                pltpu.make_async_copy(part_of(gradients[stack], i), part_of(grad_in[stack], i), g_sem.at[sem]))

    def weight_copy(stack, number):
        return pltpu.make_async_copy(weights[stack], new_w[stack], w_sem.at[number])

    for stack in ("q", "o", "d", "u"):
        for key in loads[stack]:
            for copy in load_copies(key):
                copy.start()

    barrier = pltpu.get_barrier_semaphore()
    for k in range(1, GROUP):
        pl.semaphore_signal(barrier, inc=1, device_id={"data": lax.rem(me + k, GROUP)}, device_id_type=MESH)

    part_q[...] = jnp.zeros_like(part_q)
    part_e[...] = jnp.zeros_like(part_e)

    def momentum_rows(stack, i, table, row):
        _, rows, cols, chunk, _ = STACKS[stack]
        lanes = jnp.zeros((1, 128), F32)
        for r in range(0, rows, chunk):
            at = pl.ds(r, chunk)
            mom = MOMENTUM * new_m[stack][i, at, :] + grad_in[stack][i, at, :].astype(F32)
            new_m[stack][i, at, :] = mom
            square = jnp.sum(mom * mom, axis=0, keepdims=True)
            for c in range(0, cols, 128):
                lanes = lanes + square[:, c:c + 128]
        table[pl.ds(row, 1), :] = lanes

    def push_norms(table, gathered, number):
        gathered[me] = table[...]
        for k in range(1, GROUP):
            pltpu.make_async_remote_copy(
                src_ref=table, dst_ref=gathered.at[me], send_sem=norm_send.at[number], recv_sem=norm_recv.at[number],
                device_id={"data": lax.rem(me + k, GROUP)}, device_id_type=MESH).start()

    def read_norms(gathered, den, number):
        seven = gathered.at[pl.ds(0, GROUP - 1)]
        pltpu.make_async_copy(seven, seven, norm_recv.at[number]).wait()
        total = gathered[0]
        for d in range(1, GROUP):
            total = total + gathered[d]
        total = jnp.sum(total, axis=1, keepdims=True)
        den[...] = jnp.broadcast_to(jnp.sqrt(total) + NORM_EPS, den.shape)

    def scale_rows(stack, i, den, row):
        _, rows, cols, chunk, _ = STACKS[stack]
        divisor = den[pl.ds(row, 1), 0:1]
        for r in range(0, rows, chunk):
            at = pl.ds(r, chunk)
            x = new_m[stack][i, at, :] / jnp.broadcast_to(divisor, (chunk, cols))
            if stack == "u":
                scaled[stack][i] = x.T.astype(BF16)
            else:
                scaled[stack][i, at, :] = x.astype(BF16)

    def block_of(stack, slot_ref, d):
        if stack == "u":
            return slot_ref.at[:, pl.ds(d * 128, 128)]
        rows = STACKS[stack][1]
        return slot_ref.at[pl.ds(d * rows, rows), :]

    def slot_of(stack, slot):
        if stack == "q":
            return big.at[0]
        if stack == "o":
            return big.at[0, :, pl.ds(0, 1024)]
        return ebuf.at[slot]

    def send_rows(stack, i, owner, slot):
        sem = SEM_BASE[stack] + i
        target = block_of(stack, slot_of(stack, slot), me)

        @pl.when(me != owner)
        def _():
            pltpu.make_async_remote_copy(
                src_ref=scaled[stack].at[i], dst_ref=target, send_sem=fwd_send.at[sem], recv_sem=fwd_recv.at[sem],
                device_id={"data": owner}, device_id_type=MESH).start()

        @pl.when(me == owner)
        def _():
            if stack == "u":
                for d in range(GROUP):
                    @pl.when(me == d)
                    def _():
                        ebuf[slot, :, d * 128:(d + 1) * 128] = scaled[stack][i]
            else:
                target[...] = scaled[stack][i]

    for i in range(3):
        for copy in load_copies(("q", i)):
            copy.wait()
        momentum_rows("q", i, part_q, i)
    pl.semaphore_wait(barrier, GROUP - 1)
    push_norms(part_q, gath_q, 0)

    for stack in ("o", "d", "u"):
        for copy in load_copies((stack, None)):
            copy.wait()

        @pl.loop(0, STACKS[stack][0])
        def _(i):
            momentum_rows(stack, i, part_e, STACKS[stack][4] + i)
    push_norms(part_e, gath_e, 1)

    read_norms(gath_q, den_q, 0)
    places = [place_of(kind, index) for kind, index in ORDER]
    for stack, i, owner, slot in [p for p in places if p[0] == "q"]:
        scale_rows(stack, i, den_q, i)
        send_rows(stack, i, owner, slot)
    read_norms(gath_e, den_e, 1)
    for stack in ("o", "d", "u"):
        @pl.loop(0, STACKS[stack][0])
        def _(i):
            scale_rows(stack, i, den_e, STACKS[stack][4] + i)
    for stack, i, owner, slot in [p for p in places if p[0] != "q"]:
        send_rows(stack, i, owner, slot)
    for number, stack in enumerate(("q", "o", "d", "u")):
        weight_copy(stack, number).start()

    def wait_parts(stack, slot_ref, sem):
        rows = 7 * STACKS[stack][1]
        part = slot_ref.at[:, pl.ds(0, rows)] if stack == "u" else slot_ref.at[pl.ds(0, rows), :]
        pltpu.make_async_copy(part, part, sem).wait()

    def give_back(stack, slot_ref, i, send_sem, recv_sem):
        for k in range(1, GROUP):
            dst = lax.rem(me + k, GROUP)
            pltpu.make_async_remote_copy(
                src_ref=block_of(stack, slot_ref, dst), dst_ref=back[stack].at[i], send_sem=send_sem, recv_sem=recv_sem,
                device_id={"data": dst}, device_id_type=MESH).start()

    def new_weight(w, x, stack):
        return w - LEARN_RATE * (SCALE[stack] * x.astype(F32) + DECAY * w)

    def finish(stack, i, source):
        _, rows, cols, chunk, _ = STACKS[stack]
        for r in range(0, rows, chunk):
            at = pl.ds(r, chunk)
            x = source(at)
            if stack == "u":
                x = x.astype(F32).T
            new_w[stack][i, at, :] = new_weight(new_w[stack][i, at, :], x, stack)

    for index, owner in enumerate(QKV_OWNER):
        @pl.when(me == owner)
        def _():
            wait_parts("q", big.at[0], fwd_recv.at[index])

    @pl.when((me == QKV_OWNER[0]) | (me == QKV_OWNER[1]) | (me == QKV_OWNER[2]))
    def _():
        @pl.loop(0, NS_STEPS)
        def _(it):
            now = lax.rem(it, 2)
            ns_step(big.at[now], big.at[1 - now], gram, poly, 1024, 256)

    for index, owner in enumerate(QKV_OWNER):
        @pl.when(me == owner)
        def _():
            give_back("q", big.at[1], index, ret_send.at[0], ret_recv.at[index])
            back["q"][index] = big[1, pl.ds(owner * 128, 128), :]

    for index, owner in enumerate(OUT_OWNER):
        @pl.when(me == owner)
        def _():
            wait_parts("o", big.at[0, :, pl.ds(0, 1024)], fwd_recv.at[3 + index])

    @pl.when((me == OUT_OWNER[0]) | (me == OUT_OWNER[1]) | (me == OUT_OWNER[2]))
    def _():
        @pl.loop(0, NS_STEPS)
        def _(it):
            now = lax.rem(it, 2)
            ns_step(big.at[now, :, pl.ds(0, 1024)], big.at[1 - now, :, pl.ds(0, 1024)], gram, poly, 1024, 256)

    for index, owner in enumerate(OUT_OWNER):
        @pl.when(me == owner)
        def _():
            give_back("o", big.at[1, :, pl.ds(0, 1024)], index, ret_send.at[1], ret_recv.at[3 + index])
            back["o"][index] = big[1, pl.ds(owner * 128, 128), 0:1024]

    base, count = pick(EXPERT_BASE, me), pick(EXPERT_COUNT, me)
    small_gram, small_poly = gram.at[pl.ds(0, 512), pl.ds(0, 512)], poly.at[pl.ds(0, 512), pl.ds(0, 512)]

    @pl.loop(0, count)
    def _(t):
        rank = base + t

        @pl.when(rank < N_DOWN)
        def _():
            wait_parts("d", ebuf.at[t], fwd_recv.at[6 + rank])

        @pl.when(rank >= N_DOWN)
        def _():
            wait_parts("u", ebuf.at[t], fwd_recv.at[6 + rank])

        @pl.loop(0, NS_STEPS)
        def _(it):
            src = jnp.where(it == 0, t, MAX_EXPERTS + lax.rem(it + 1, 2))
            dst = jnp.where(it == NS_STEPS - 1, t, MAX_EXPERTS + lax.rem(it, 2))
            ns_step(ebuf.at[src], ebuf.at[dst], small_gram, small_poly, 512, 256)

        @pl.when(rank < N_DOWN)
        def _():
            give_back("d", ebuf.at[t], rank, ret_send.at[2 + t], ret_recv.at[6 + rank])
            back["d"][rank] = ebuf[t, pl.ds(pl.multiple_of(me * 64, 64), 64), :]

        @pl.when(rank >= N_DOWN)
        def _():
            give_back("u", ebuf.at[t], rank - N_DOWN, ret_send.at[2 + t], ret_recv.at[6 + rank])
            for d in range(GROUP):
                if EXPERT_BASE[d] + EXPERT_COUNT[d] > N_DOWN and EXPERT_COUNT[d]:
                    @pl.when(me == d)
                    def _():
                        back["u"][rank - N_DOWN] = ebuf[t, :, d * 128:(d + 1) * 128]

    for number, stack in enumerate(("q", "o", "d", "u")):
        weight_copy(stack, number).wait()
    owners = {(stack, i): owner for stack, i, owner, _ in places}
    for stack, i in RETURNS:
        owner, sem = owners[stack, i], SEM_BASE[stack] + i

        @pl.when(me != owner)
        def _():
            row = back[stack].at[i]
            pltpu.make_async_copy(row, row, ret_recv.at[sem]).wait()

        if stack == "u":
            finish(stack, i, lambda at: back["u"][i])
        else:
            finish(stack, i, lambda at: back[stack][i, at, :])

    for number, (table, gathered) in enumerate(((part_q, gath_q), (part_e, gath_e))):
        seven = gathered.at[pl.ds(0, GROUP - 1)]
        pltpu.make_async_copy(seven, seven, norm_send.at[number]).wait()
    for stack, i, owner, slot in places:
        @pl.when(me != owner)
        def _():
            block = scaled[stack].at[i]
            pltpu.make_async_copy(block, block, fwd_send.at[SEM_BASE[stack] + i]).wait()
    for owner in QKV_OWNER:
        @pl.when(me == owner)
        def _():
            wait_parts("q", big.at[1], ret_send.at[0])
    for owner in OUT_OWNER:
        @pl.when(me == owner)
        def _():
            wait_parts("o", big.at[1, :, pl.ds(0, 1024)], ret_send.at[1])

    @pl.loop(0, count)
    def _(t):
        @pl.when(base + t < N_DOWN)
        def _():
            wait_parts("d", ebuf.at[t], ret_send.at[2 + t])

        @pl.when(base + t >= N_DOWN)
        def _():
            wait_parts("u", ebuf.at[t], ret_send.at[2 + t])


OUT_SPACE = pltpu.VMEM


def solution(mesh):
    row_spec = P("stage", "data", None)

    def local_step(*args):
        shapes = [args[k].shape for k in (0, 3, 6, 9) for _ in range(2)]
        any_space = pl.BlockSpec(memory_space=pl.ANY)
        return tuple(pl.pallas_call(
            kernel,
            out_shape=[OUT_SPACE(shape, F32) for shape in shapes],
            in_specs=[any_space] * 12,
            out_specs=[pl.BlockSpec(memory_space=OUT_SPACE)] * 8,
            scratch_shapes=[
                pltpu.VMEM((2, 1024, 2048), BF16),
                pltpu.VMEM((MAX_EXPERTS + 2, 512, 1024), BF16),
                pltpu.VMEM((1024, 1024), BF16),
                pltpu.VMEM((1024, 1024), BF16),
                pltpu.VMEM((3, 128, 2048), BF16),
                pltpu.VMEM((3, 128, 1024), BF16),
                pltpu.VMEM((12, 64, 1024), BF16),
                pltpu.VMEM((12, 512, 128), BF16),
                pltpu.VMEM((3, 128, 2048), BF16),
                pltpu.VMEM((3, 128, 1024), BF16),
                pltpu.VMEM((12, 64, 1024), BF16),
                pltpu.VMEM((12, 128, 512), BF16),
                pltpu.VMEM((12, 512, 128), BF16),
                pltpu.VMEM((8, 128), F32),
                pltpu.VMEM((32, 128), F32),
                pltpu.VMEM((GROUP, 8, 128), F32),
                pltpu.VMEM((GROUP, 32, 128), F32),
                pltpu.VMEM((8, 128), F32),
                pltpu.VMEM((32, 128), F32),
                pltpu.SemaphoreType.DMA((6,)),
                pltpu.SemaphoreType.DMA((6,)),
                pltpu.SemaphoreType.DMA((4,)),
                pltpu.SemaphoreType.DMA((2,)),
                pltpu.SemaphoreType.DMA((2,)),
                pltpu.SemaphoreType.DMA((30,)),
                pltpu.SemaphoreType.DMA((30,)),
                pltpu.SemaphoreType.DMA((2 + MAX_EXPERTS,)),
                pltpu.SemaphoreType.DMA((30,)),
            ],
            compiler_params=pltpu.CompilerParams(
                collective_id=0, has_side_effects=True, vmem_limit_bytes=VMEM_LIMIT),
        )(*args))

    return jax.shard_map(local_step, mesh=mesh, in_specs=(row_spec,) * 12, out_specs=(row_spec,) * 8, check_vma=False)
```

time: 309 us -> 262 us (0.85)
  other arithmetic: 35.1 us -> 0 us
  blocking collectives: 10.2 us -> 0 us
  local copies, waits for them, and re-layouts: 15.6 us -> 12.3 us
    sub x4 -> x0, other arithmetic: 15.8 us -> none  [local_step(): weight - LEARN_RATE * (rms_scale * back.astype(F32) + DECAY * weight)]
    reduce_sum x4 -> x0, other arithmetic: 11.4 us -> none  [local_step(): sums.append(jnp.sum(new_mom * new_mom, axis=(1, 2)))]
    psum x1 -> x0, blocking collectives: 10.2 us -> none  [local_step(): sums = lax.psum(tuple(sums), 'data')]
    convert_element_type x3 -> x0, other arithmetic: 6.32 us -> none  [local_step(): (m / (jnp.sqrt(s)[:, None, None] + NORM_EPS)).astype(BF16)]
    unnamed x23 -> x8, local copies, waits for them, and re-layouts: 15.6 us -> 12.3 us
where the time goes in v2:
time: 262 us
  Pallas kernels  249 us (95%)
  local copies, waits for them, and re-layouts  12.3 us (5%)
    pallas_call x1, Pallas kernels, local_step(): pl.pallas_call(kernel, out_shape=[OUT_SPACE(shape, F32) for shape in shap...  249 us
    unnamed x8, local copies, waits for them, and re-layouts  12.3 us

profile of v2, /device:TPU:9, one launch (start us, length us, event | category | flops | bytes accessed | tf_op | source)
XLA Modules:
  0.0 262.1 jit_solution(17044456065118277359)
XLA Ops:
  0.6 249.2 %shard_map.179 = (f32[3,128,2048]{2,1,0:T(8,128)S(1)}, f32[3,128,2048]{2,1,0:T(8,128)S(1)}, f32[3,128,1024]{2,1,0:T(8,128)S(1)}, f32[3,128,1024]{2,1,0:T(8,128)S...) custom-call(f32[3,128,2048]{2,1,0:T(8,128)} %w_q.1, ...), custom_call_target="tpu_custom_call" | custom-call | tf_op jit(solution)/shard_map/pallas_call | solution.py:420
  249.8 1.7 copy.28
  251.5 1.1 copy.30
  252.7 1.1 copy.31
  253.8 1.7 copy.29
  255.5 1.7 copy.32
  257.1 1.7 copy.33
  258.8 1.7 copy.34
  260.5 1.7 copy.35

commit v3 on v2

--- a/solution.py
+++ b/solution.py
@@ -114,7 +114,7 @@
         stack, position, owner, slot = place_of(kind, index)
         total = 4 if kind == "q" else EXPERT_COUNT[owner] + (2 if owner in OUT_OWNER else 0)
         if kind == "q":
-            done = 0.6 * total
+            done = 0.85 * total
         else:
             done = 2 if kind == "o" else slot + 1 + (2 if owner in OUT_OWNER else 0)
         keys.append((done / total, len(keys), stack, position))
@@ -154,10 +154,9 @@
     def weight_copy(stack, number):
         return pltpu.make_async_copy(weights[stack], new_w[stack], w_sem.at[number])
 
-    for stack in ("q", "o", "d", "u"):
-        for key in loads[stack]:
-            for copy in load_copies(key):
-                copy.start()
+    for key in loads["q"]:
+        for copy in load_copies(key):
+            copy.start()
 
     barrier = pltpu.get_barrier_semaphore()
     for k in range(1, GROUP):
@@ -238,36 +237,44 @@
             else:
                 target[...] = scaled[stack][i]
 
+    def momentum_stack(stack):
+        for copy in load_copies((stack, None)):
+            copy.wait()
+
+        @pl.loop(0, STACKS[stack][0])
+        def _(i):
+            momentum_rows(stack, i, part_e, STACKS[stack][4] + i)
+
+    def scale_stack(stack):
+        @pl.loop(0, STACKS[stack][0])
+        def _(i):
+            scale_rows(stack, i, den_e, STACKS[stack][4] + i)
+
     for i in range(3):
         for copy in load_copies(("q", i)):
             copy.wait()
         momentum_rows("q", i, part_q, i)
+    for stack in ("o", "d", "u"):
+        for copy in load_copies((stack, None)):
+            copy.start()
     pl.semaphore_wait(barrier, GROUP - 1)
     push_norms(part_q, gath_q, 0)
-
-    for stack in ("o", "d", "u"):
-        for copy in load_copies((stack, None)):
-            copy.wait()
-
-        @pl.loop(0, STACKS[stack][0])
-        def _(i):
-            momentum_rows(stack, i, part_e, STACKS[stack][4] + i)
-    push_norms(part_e, gath_e, 1)
-
+    momentum_stack("o")
+    momentum_stack("d")
     read_norms(gath_q, den_q, 0)
     places = [place_of(kind, index) for kind, index in ORDER]
     for stack, i, owner, slot in [p for p in places if p[0] == "q"]:
         scale_rows(stack, i, den_q, i)
         send_rows(stack, i, owner, slot)
+    momentum_stack("u")
+    push_norms(part_e, gath_e, 1)
+    for number, stack in enumerate(("q", "o", "d", "u")):
+        weight_copy(stack, number).start()
     read_norms(gath_e, den_e, 1)
     for stack in ("o", "d", "u"):
-        @pl.loop(0, STACKS[stack][0])
-        def _(i):
-            scale_rows(stack, i, den_e, STACKS[stack][4] + i)
+        scale_stack(stack)
     for stack, i, owner, slot in [p for p in places if p[0] != "q"]:
         send_rows(stack, i, owner, slot)
-    for number, stack in enumerate(("q", "o", "d", "u")):
-        weight_copy(stack, number).start()
 
     def wait_parts(stack, slot_ref, sem):
         rows = 7 * STACKS[stack][1]
@@ -411,13 +418,21 @@
 OUT_SPACE = pltpu.VMEM
 
 
+def store_kernel(*refs):
+    copies = [pltpu.make_async_copy(refs[k], refs[8 + k], refs[16].at[k]) for k in range(8)]
+    for copy in copies:
+        copy.start()
+    for copy in copies:
+        copy.wait()
+
+
 def solution(mesh):
     row_spec = P("stage", "data", None)
 
     def local_step(*args):
         shapes = [args[k].shape for k in (0, 3, 6, 9) for _ in range(2)]
         any_space = pl.BlockSpec(memory_space=pl.ANY)
-        return tuple(pl.pallas_call(
+        kept = pl.pallas_call(
             kernel,
             out_shape=[OUT_SPACE(shape, F32) for shape in shapes],
             in_specs=[any_space] * 12,
@@ -454,6 +469,14 @@
             ],
             compiler_params=pltpu.CompilerParams(
                 collective_id=0, has_side_effects=True, vmem_limit_bytes=VMEM_LIMIT),
-        )(*args))
+        )(*args)
+        return tuple(pl.pallas_call(
+            store_kernel,
+            out_shape=[jax.ShapeDtypeStruct(shape, F32) for shape in shapes],
+            in_specs=[any_space] * 8,
+            out_specs=[any_space] * 8,
+            scratch_shapes=[pltpu.SemaphoreType.DMA((8,))],
+            compiler_params=pltpu.CompilerParams(vmem_limit_bytes=1024 * 1024),
+        )(*kept))
 
     return jax.shard_map(local_step, mesh=mesh, in_specs=(row_spec,) * 12, out_specs=(row_spec,) * 8, check_vma=False)

time: 262 us -> 290 us (1.11)
  Pallas kernels: 249 us -> 288 us
  local copies, waits for them, and re-layouts: 12.3 us -> 0 us
    pallas_call x1, Pallas kernels: 249 us -> 281 us  [local_step(): pl.pallas_call(kernel, out_shape=[OUT_SPACE(shape, F32) for shape in shap...]
    unnamed x8 -> x0, local copies, waits for them, and re-layouts: 12.3 us -> none
    pallas_call x0 -> x1, Pallas kernels: none -> 7.59 us  [local_step(): pl.pallas_call(store_kernel, out_shape=[jax.ShapeDtypeStruct(shape, F32)...]
where the time goes in v3:
time: 290 us; the launch traced here: 289 us
  Pallas kernels  288 us (99%)
    pallas_call x1, Pallas kernels, local_step(): pl.pallas_call(kernel, out_shape=[OUT_SPACE(shape, F32) for shape in shap...  281 us
    pallas_call x1, Pallas kernels, local_step(): pl.pallas_call(store_kernel, out_shape=[jax.ShapeDtypeStruct(shape, F32)...  7.59 us

profile of v3, /device:TPU:9, one launch (start us, length us, event | category | flops | bytes accessed | tf_op | source)
XLA Modules:
  0.0 289.2 jit_solution(3814280983551380857)
XLA Ops:
  0.6 280.8 %shard_map.179 = (f32[3,128,2048]{2,1,0:T(8,128)S(1)}, f32[3,128,2048]{2,1,0:T(8,128)S(1)}, f32[3,128,1024]{2,1,0:T(8,128)S(1)}, f32[3,128,1024]{2,1,0:T(8,128)S...) custom-call(f32[3,128,2048]{2,1,0:T(8,128)} %w_q.1, ...), custom_call_target="tpu_custom_call" | custom-call | tf_op jit(solution)/shard_map/pallas_call | solution.py:435
  281.4 7.6 %shard_map.180 = (f32[3,128,2048]{2,1,0:T(8,128)}, f32[3,128,2048]{2,1,0:T(8,128)}, f32[3,128,1024]{2,1,0:T(8,128)}, f32[3,128,1024]{2,1,0:T(8,128)}, f32[12,128...) custom-call(f32[3,128,2048]{2,1,0:T(8,128)S(1)} %get-tuple-element.16.refs_0_, ...), custom_call_target="tpu_custom_call" | custom-call | tf_op jit(solution)/shard_map/pallas_call | solution.py:473

commit v4 on v3

--- a/solution.py
+++ b/solution.py
@@ -253,21 +253,22 @@
     for i in range(3):
         for copy in load_copies(("q", i)):
             copy.wait()
+        if i == 0:
+            for stack in ("o", "d", "u"):
+                for copy in load_copies((stack, None)):
+                    copy.start()
         momentum_rows("q", i, part_q, i)
-    for stack in ("o", "d", "u"):
-        for copy in load_copies((stack, None)):
-            copy.start()
     pl.semaphore_wait(barrier, GROUP - 1)
     push_norms(part_q, gath_q, 0)
     momentum_stack("o")
     momentum_stack("d")
+    momentum_stack("u")
+    push_norms(part_e, gath_e, 1)
     read_norms(gath_q, den_q, 0)
     places = [place_of(kind, index) for kind, index in ORDER]
     for stack, i, owner, slot in [p for p in places if p[0] == "q"]:
         scale_rows(stack, i, den_q, i)
         send_rows(stack, i, owner, slot)
-    momentum_stack("u")
-    push_norms(part_e, gath_e, 1)
     for number, stack in enumerate(("q", "o", "d", "u")):
         weight_copy(stack, number).start()
     read_norms(gath_e, den_e, 1)

time: 290 us -> 258 us (0.89)
  Pallas kernels: 288 us -> 257 us
    pallas_call x1, Pallas kernels: 281 us -> 249 us  [local_step(): pl.pallas_call(kernel, out_shape=[OUT_SPACE(shape, F32) for shape in shap...]
where the time goes in v4:
time: 258 us
  Pallas kernels  257 us (100%)
    pallas_call x1, Pallas kernels, local_step(): pl.pallas_call(kernel, out_shape=[OUT_SPACE(shape, F32) for shape in shap...  249 us
    pallas_call x1, Pallas kernels, local_step(): pl.pallas_call(store_kernel, out_shape=[jax.ShapeDtypeStruct(shape, F32)...  7.59 us

profile of v4, /device:TPU:9, one launch (start us, length us, event | category | flops | bytes accessed | tf_op | source)
XLA Modules:
  0.0 257.7 jit_solution(8893083607300052403)
XLA Ops:
  0.6 249.3 %shard_map.179 = (f32[3,128,2048]{2,1,0:T(8,128)S(1)}, f32[3,128,2048]{2,1,0:T(8,128)S(1)}, f32[3,128,1024]{2,1,0:T(8,128)S(1)}, f32[3,128,1024]{2,1,0:T(8,128)S...) custom-call(f32[3,128,2048]{2,1,0:T(8,128)} %w_q.1, ...), custom_call_target="tpu_custom_call" | custom-call | tf_op jit(solution)/shard_map/pallas_call | solution.py:436
  250.0 7.6 %shard_map.180 = (f32[3,128,2048]{2,1,0:T(8,128)}, f32[3,128,2048]{2,1,0:T(8,128)}, f32[3,128,1024]{2,1,0:T(8,128)}, f32[3,128,1024]{2,1,0:T(8,128)}, f32[12,128...) custom-call(f32[3,128,2048]{2,1,0:T(8,128)S(1)} %get-tuple-element.16.refs_0_, ...), custom_call_target="tpu_custom_call" | custom-call | tf_op jit(solution)/shard_map/pallas_call | solution.py:474

commit v5 on v4

--- a/solution.py
+++ b/solution.py
@@ -22,10 +22,10 @@
 F32 = jnp.float32
 BF16 = jnp.bfloat16
 
-QKV_OWNER = (0, 1, 7)
-OUT_OWNER = (2, 4, 6)
-EXPERT_COUNT = (0, 0, 3, 8, 3, 7, 3, 0)
-EXPERT_BASE = (0, 0, 0, 3, 11, 14, 21, 24)
+QKV_OWNER = (2, 0, 5)
+OUT_OWNER = (1, 6, 7)
+EXPERT_COUNT = (0, 0, 7, 4, 7, 3, 1, 2)
+EXPERT_BASE = tuple(sum(EXPERT_COUNT[:d]) for d in range(GROUP))
 EXPERT_OWNER = tuple(d for d in range(GROUP) for _ in range(EXPERT_COUNT[d]))
 N_DOWN = 12
 MAX_EXPERTS = 8
@@ -43,7 +43,7 @@
         slots = []
         for d in devices:
             for t in range(EXPERT_COUNT[d]):
-                slots.append(((t + 0.5) / EXPERT_COUNT[d], d, t))
+                slots.append(((t + 0.5) / EXPERT_COUNT[d] + (d in QKV_OWNER), d, t))
         for _, d, t in sorted(slots):
             halves[half].append(("e", EXPERT_BASE[d] + t))
     order, sent, place = [], [0, 0], [0, 0]
@@ -110,14 +110,11 @@
 
 def return_order():
     keys = []
-    for kind, index in ORDER:
+    for number, (kind, index) in enumerate(ORDER):
         stack, position, owner, slot = place_of(kind, index)
-        total = 4 if kind == "q" else EXPERT_COUNT[owner] + (2 if owner in OUT_OWNER else 0)
-        if kind == "q":
-            done = 0.85 * total
-        else:
-            done = 2 if kind == "o" else slot + 1 + (2 if owner in OUT_OWNER else 0)
-        keys.append((done / total, len(keys), stack, position))
+        before = 75 * (owner in QKV_OWNER) + 42 * (owner in OUT_OWNER)
+        work = before if kind != "e" else before + 10 * (slot + 1)
+        keys.append((max(work, 2 * number) + (40 if kind == "q" else 0), len(keys), stack, position))
     return [(stack, position) for _, _, stack, position in sorted(keys)]
 
 
@@ -283,8 +280,9 @@
         pltpu.make_async_copy(part, part, sem).wait()
 
     def give_back(stack, slot_ref, i, send_sem, recv_sem):
-        for k in range(1, GROUP):
-            dst = lax.rem(me + k, GROUP)
+        half = me // 4
+        crossing = [(1 - half) * 4 + k for k in range(4)]
+        for dst in crossing + [half * 4 + lax.rem(me + k, 4) for k in range(1, 4)]:
             pltpu.make_async_remote_copy(
                 src_ref=block_of(stack, slot_ref, dst), dst_ref=back[stack].at[i], send_sem=send_sem, recv_sem=recv_sem,
                 device_id={"data": dst}, device_id_type=MESH).start()

time: 258 us -> 259 us (level)
  no operation moved by 1% of the time
where the time goes in v5:
time: 259 us
  Pallas kernels  258 us (100%)
    pallas_call x1, Pallas kernels, local_step(): pl.pallas_call(kernel, out_shape=[OUT_SPACE(shape, F32) for shape in shap...  250 us
    pallas_call x1, Pallas kernels, local_step(): pl.pallas_call(store_kernel, out_shape=[jax.ShapeDtypeStruct(shape, F32)...  7.59 us

profile of v5, /device:TPU:9, one launch (start us, length us, event | category | flops | bytes accessed | tf_op | source)
XLA Modules:
  0.0 258.8 jit_solution(9932180106732555444)
XLA Ops:
  0.6 250.4 %shard_map.179 = (f32[3,128,2048]{2,1,0:T(8,128)S(1)}, f32[3,128,2048]{2,1,0:T(8,128)S(1)}, f32[3,128,1024]{2,1,0:T(8,128)S(1)}, f32[3,128,1024]{2,1,0:T(8,128)S...) custom-call(f32[3,128,2048]{2,1,0:T(8,128)} %w_q.1, ...), custom_call_target="tpu_custom_call" | custom-call | tf_op jit(solution)/shard_map/pallas_call | solution.py:434
  251.1 7.6 %shard_map.180 = (f32[3,128,2048]{2,1,0:T(8,128)}, f32[3,128,2048]{2,1,0:T(8,128)}, f32[3,128,1024]{2,1,0:T(8,128)}, f32[3,128,1024]{2,1,0:T(8,128)}, f32[12,128...) custom-call(f32[3,128,2048]{2,1,0:T(8,128)S(1)} %get-tuple-element.16.refs_0_, ...), custom_call_target="tpu_custom_call" | custom-call | tf_op jit(solution)/shard_map/pallas_call | solution.py:472

commit v6 on v5

--- a/solution.py
+++ b/solution.py
@@ -22,9 +22,9 @@
 F32 = jnp.float32
 BF16 = jnp.bfloat16
 
-QKV_OWNER = (2, 0, 5)
-OUT_OWNER = (1, 6, 7)
-EXPERT_COUNT = (0, 0, 7, 4, 7, 3, 1, 2)
+QKV_OWNER = (2, 1, 5)
+OUT_OWNER = (3, 4, 7)
+EXPERT_COUNT = (2, 0, 4, 5, 8, 1, 4, 0)
 EXPERT_BASE = tuple(sum(EXPERT_COUNT[:d]) for d in range(GROUP))
 EXPERT_OWNER = tuple(d for d in range(GROUP) for _ in range(EXPERT_COUNT[d]))
 N_DOWN = 12
@@ -35,7 +35,7 @@
 def send_order():
     halves = ([], [])
     sizes = {"q": 4, "o": 2, "e": 1}
-    for kind, owners in (("q", QKV_OWNER), ("o", OUT_OWNER)):
+    for kind, owners in (("o", OUT_OWNER), ("q", QKV_OWNER)):
         for index, owner in enumerate(owners):
             halves[owner // 4].append((kind, index))
     for half in range(2):
@@ -92,7 +92,7 @@
         dst[rows, :] = (COEF_A * src[rows, :].astype(F32) + product).astype(BF16)
 
 
-STACKS = {"q": (3, 128, 2048, 32, 0), "o": (3, 128, 1024, 64, 0), "d": (12, 64, 1024, 64, 3), "u": (12, 128, 512, 128, 15)}
+STACKS = {"q": (3, 128, 2048, 32, 0), "o": (3, 128, 1024, 64, 0), "d": (12, 64, 1024, 64, 0), "u": (12, 128, 512, 128, 12)}
 SCALE = {"q": RMS_MATCH * math.sqrt(2048), "o": RMS_MATCH * math.sqrt(1024),
          "d": RMS_MATCH * math.sqrt(1024), "u": RMS_MATCH * math.sqrt(1024)}
 SEM_BASE = {"q": 0, "o": 3, "d": 6, "u": 18}
@@ -124,7 +124,7 @@
 def kernel(w_q, m_q, g_q, w_o, m_o, g_o, w_u, m_u, g_u, w_d, m_d, g_d,
            nw_q, nm_q, nw_o, nm_o, nw_u, nm_u, nw_d, nm_d,
            big, ebuf, gram, poly, xs_q, xs_o, xs_d, xs_u, bk_q, bk_o, bk_d, gs_u, bk_u,
-           part_q, part_e, gath_q, gath_e, den_q, den_e,
+           part, gath, den,
            m_sem, g_sem, w_sem, norm_send, norm_recv, fwd_send, fwd_recv, ret_send, ret_recv):
     me = lax.axis_index("data")
     weights = {"q": w_q, "o": w_o, "d": w_d, "u": w_u}
@@ -151,7 +151,7 @@
     def weight_copy(stack, number):
         return pltpu.make_async_copy(weights[stack], new_w[stack], w_sem.at[number])
 
-    for key in loads["q"]:
+    for key in loads["o"] + loads["q"]:
         for copy in load_copies(key):
             copy.start()
 
@@ -159,10 +159,10 @@
     for k in range(1, GROUP):
         pl.semaphore_signal(barrier, inc=1, device_id={"data": lax.rem(me + k, GROUP)}, device_id_type=MESH)
 
-    part_q[...] = jnp.zeros_like(part_q)
-    part_e[...] = jnp.zeros_like(part_e)
-
-    def momentum_rows(stack, i, table, row):
+    part[...] = jnp.zeros_like(part)
+    lane = lax.broadcasted_iota(jnp.int32, (8, 128), 1)
+
+    def momentum_rows(stack, i, number, column):
         _, rows, cols, chunk, _ = STACKS[stack]
         lanes = jnp.zeros((1, 128), F32)
         for r in range(0, rows, chunk):
@@ -172,27 +172,27 @@
             square = jnp.sum(mom * mom, axis=0, keepdims=True)
             for c in range(0, cols, 128):
                 lanes = lanes + square[:, c:c + 128]
-        table[pl.ds(row, 1), :] = lanes
-
-    def push_norms(table, gathered, number):
-        gathered[me] = table[...]
+        total = jnp.sum(lanes, axis=1, keepdims=True)
+        part[number] = jnp.where(lane == column, jnp.broadcast_to(total, (8, 128)), part[number])
+
+    def push_norms(number):
+        gath[number, me] = part[number]
         for k in range(1, GROUP):
             pltpu.make_async_remote_copy(
-                src_ref=table, dst_ref=gathered.at[me], send_sem=norm_send.at[number], recv_sem=norm_recv.at[number],
-                device_id={"data": lax.rem(me + k, GROUP)}, device_id_type=MESH).start()
-
-    def read_norms(gathered, den, number):
-        seven = gathered.at[pl.ds(0, GROUP - 1)]
+                src_ref=part.at[number], dst_ref=gath.at[number, me], send_sem=norm_send.at[number],
+                recv_sem=norm_recv.at[number], device_id={"data": lax.rem(me + k, GROUP)}, device_id_type=MESH).start()
+
+    def read_norms(number):
+        seven = gath.at[number, pl.ds(0, GROUP - 1)]
         pltpu.make_async_copy(seven, seven, norm_recv.at[number]).wait()
-        total = gathered[0]
+        total = gath[number, 0]
         for d in range(1, GROUP):
-            total = total + gathered[d]
-        total = jnp.sum(total, axis=1, keepdims=True)
-        den[...] = jnp.broadcast_to(jnp.sqrt(total) + NORM_EPS, den.shape)
-
-    def scale_rows(stack, i, den, row):
+            total = total + gath[number, d]
+        den[number] = jnp.sqrt(total) + NORM_EPS
+
+    def scale_rows(stack, i, number, column):
         _, rows, cols, chunk, _ = STACKS[stack]
-        divisor = den[pl.ds(row, 1), 0:1]
+        divisor = jnp.sum(jnp.where(lane[:1] == column, den[number, 0:1, :], 0.0), axis=1, keepdims=True)
         for r in range(0, rows, chunk):
             at = pl.ds(r, chunk)
             x = new_m[stack][i, at, :] / jnp.broadcast_to(divisor, (chunk, cols))
@@ -234,45 +234,50 @@
             else:
                 target[...] = scaled[stack][i]
 
-    def momentum_stack(stack):
+    def momentum_stack(stack, number):
         for copy in load_copies((stack, None)):
             copy.wait()
 
         @pl.loop(0, STACKS[stack][0])
         def _(i):
-            momentum_rows(stack, i, part_e, STACKS[stack][4] + i)
-
-    def scale_stack(stack):
-        @pl.loop(0, STACKS[stack][0])
-        def _(i):
-            scale_rows(stack, i, den_e, STACKS[stack][4] + i)
-
+            momentum_rows(stack, i, number, STACKS[stack][4] + i)
+
+    places = [place_of(kind, index) for kind, index in ORDER]
+
+    def scale_and_send(stack, number):
+        for kind, i, owner, slot in places:
+            if kind == stack:
+                scale_rows(stack, i, number, i)
+                send_rows(stack, i, owner, slot)
+
+    momentum_stack("o", 0)
+    pl.semaphore_wait(barrier, GROUP - 1)
+    push_norms(0)
+    for stack in ("d", "u"):
+        for copy in load_copies((stack, None)):
+            copy.start()
     for i in range(3):
         for copy in load_copies(("q", i)):
             copy.wait()
-        if i == 0:
-            for stack in ("o", "d", "u"):
-                for copy in load_copies((stack, None)):
-                    copy.start()
-        momentum_rows("q", i, part_q, i)
-    pl.semaphore_wait(barrier, GROUP - 1)
-    push_norms(part_q, gath_q, 0)
-    momentum_stack("o")
-    momentum_stack("d")
-    momentum_stack("u")
-    push_norms(part_e, gath_e, 1)
-    read_norms(gath_q, den_q, 0)
-    places = [place_of(kind, index) for kind, index in ORDER]
-    for stack, i, owner, slot in [p for p in places if p[0] == "q"]:
-        scale_rows(stack, i, den_q, i)
-        send_rows(stack, i, owner, slot)
+        momentum_rows("q", i, 1, i)
+    push_norms(1)
+    momentum_stack("d", 2)
+    read_norms(0)
+    scale_and_send("o", 0)
+    momentum_stack("u", 2)
+    push_norms(2)
+    read_norms(1)
+    scale_and_send("q", 1)
     for number, stack in enumerate(("q", "o", "d", "u")):
         weight_copy(stack, number).start()
-    read_norms(gath_e, den_e, 1)
-    for stack in ("o", "d", "u"):
-        scale_stack(stack)
-    for stack, i, owner, slot in [p for p in places if p[0] != "q"]:
-        send_rows(stack, i, owner, slot)
+    read_norms(2)
+    for stack in ("d", "u"):
+        @pl.loop(0, STACKS[stack][0])
+        def _(i):
+            scale_rows(stack, i, 2, STACKS[stack][4] + i)
+    for stack, i, owner, slot in places:
+        if stack in "du":
+            send_rows(stack, i, owner, slot)
 
     def wait_parts(stack, slot_ref, sem):
         rows = 7 * STACKS[stack][1]
@@ -386,8 +391,8 @@
         else:
             finish(stack, i, lambda at: back[stack][i, at, :])
 
-    for number, (table, gathered) in enumerate(((part_q, gath_q), (part_e, gath_e))):
-        seven = gathered.at[pl.ds(0, GROUP - 1)]
+    for number in range(3):
+        seven = gath.at[number, pl.ds(0, GROUP - 1)]
         pltpu.make_async_copy(seven, seven, norm_send.at[number]).wait()
     for stack, i, owner, slot in places:
         @pl.when(me != owner)
@@ -450,17 +455,14 @@
                 pltpu.VMEM((12, 64, 1024), BF16),
                 pltpu.VMEM((12, 128, 512), BF16),
                 pltpu.VMEM((12, 512, 128), BF16),
-                pltpu.VMEM((8, 128), F32),
-                pltpu.VMEM((32, 128), F32),
-                pltpu.VMEM((GROUP, 8, 128), F32),
-                pltpu.VMEM((GROUP, 32, 128), F32),
-                pltpu.VMEM((8, 128), F32),
-                pltpu.VMEM((32, 128), F32),
+                pltpu.VMEM((3, 8, 128), F32),
+                pltpu.VMEM((3, GROUP, 8, 128), F32),
+                pltpu.VMEM((3, 8, 128), F32),
                 pltpu.SemaphoreType.DMA((6,)),
                 pltpu.SemaphoreType.DMA((6,)),
                 pltpu.SemaphoreType.DMA((4,)),
-                pltpu.SemaphoreType.DMA((2,)),
-                pltpu.SemaphoreType.DMA((2,)),
+                pltpu.SemaphoreType.DMA((3,)),
+                pltpu.SemaphoreType.DMA((3,)),
                 pltpu.SemaphoreType.DMA((30,)),
                 pltpu.SemaphoreType.DMA((30,)),
                 pltpu.SemaphoreType.DMA((2 + MAX_EXPERTS,)),

time: 259 us -> 256 us (0.988)
  Pallas kernels: 258 us -> 255 us
    pallas_call x1, Pallas kernels: 250 us -> 247 us  [local_step(): pl.pallas_call(kernel, out_shape=[OUT_SPACE(shape, F32) for shape in shap...]
where the time goes in v6:
time: 256 us
  Pallas kernels  255 us (100%)
    pallas_call x1, Pallas kernels, local_step(): pl.pallas_call(kernel, out_shape=[OUT_SPACE(shape, F32) for shape in shap...  247 us
    pallas_call x1, Pallas kernels, local_step(): pl.pallas_call(store_kernel, out_shape=[jax.ShapeDtypeStruct(shape, F32)...  7.59 us

profile of v6, /device:TPU:9, one launch (start us, length us, event | category | flops | bytes accessed | tf_op | source)
XLA Modules:
  0.0 255.8 jit_solution(13230702799542786260)
XLA Ops:
  0.6 247.4 %shard_map.179 = (f32[3,128,2048]{2,1,0:T(8,128)S(1)}, f32[3,128,2048]{2,1,0:T(8,128)S(1)}, f32[3,128,1024]{2,1,0:T(8,128)S(1)}, f32[3,128,1024]{2,1,0:T(8,128)S...) custom-call(f32[3,128,2048]{2,1,0:T(8,128)} %w_q.1, ...), custom_call_target="tpu_custom_call" | custom-call | tf_op jit(solution)/shard_map/pallas_call | solution.py:439
  248.0 7.6 %shard_map.180 = (f32[3,128,2048]{2,1,0:T(8,128)}, f32[3,128,2048]{2,1,0:T(8,128)}, f32[3,128,1024]{2,1,0:T(8,128)}, f32[3,128,1024]{2,1,0:T(8,128)}, f32[12,128...) custom-call(f32[3,128,2048]{2,1,0:T(8,128)S(1)} %get-tuple-element.16.refs_0_, ...), custom_call_target="tpu_custom_call" | custom-call | tf_op jit(solution)/shard_map/pallas_call | solution.py:474

commit v7 on v6

--- a/solution.py
+++ b/solution.py
@@ -110,11 +110,10 @@
 
 def return_order():
     keys = []
-    for number, (kind, index) in enumerate(ORDER):
+    for kind, index in ORDER:
         stack, position, owner, slot = place_of(kind, index)
-        before = 75 * (owner in QKV_OWNER) + 42 * (owner in OUT_OWNER)
-        work = before if kind != "e" else before + 10 * (slot + 1)
-        keys.append((max(work, 2 * number) + (40 if kind == "q" else 0), len(keys), stack, position))
+        held = 4 * (owner in QKV_OWNER) + 2 * (owner in OUT_OWNER)
+        keys.append((held + (slot + 1 if kind == "e" else 0), len(keys), stack, position))
     return [(stack, position) for _, _, stack, position in sorted(keys)]
 
 
@@ -237,7 +236,9 @@
     def momentum_stack(stack, number):
         for copy in load_copies((stack, None)):
             copy.wait()
-
+        momentum_loop(stack, number)
+
+    def momentum_loop(stack, number):
         @pl.loop(0, STACKS[stack][0])
         def _(i):
             momentum_rows(stack, i, number, STACKS[stack][4] + i)
@@ -250,12 +251,14 @@
                 scale_rows(stack, i, number, i)
                 send_rows(stack, i, owner, slot)
 
-    momentum_stack("o", 0)
-    pl.semaphore_wait(barrier, GROUP - 1)
-    push_norms(0)
+    for copy in load_copies(("o", None)):
+        copy.wait()
     for stack in ("d", "u"):
         for copy in load_copies((stack, None)):
             copy.start()
+    momentum_loop("o", 0)
+    pl.semaphore_wait(barrier, GROUP - 1)
+    push_norms(0)
     for i in range(3):
         for copy in load_copies(("q", i)):
             copy.wait()

time: 256 us -> 256 us (level)
  no operation moved by 1% of the time
where the time goes in v7:
time: 256 us
  Pallas kernels  255 us (100%)
    pallas_call x1, Pallas kernels, local_step(): pl.pallas_call(kernel, out_shape=[OUT_SPACE(shape, F32) for shape in shap...  247 us
    pallas_call x1, Pallas kernels, local_step(): pl.pallas_call(store_kernel, out_shape=[jax.ShapeDtypeStruct(shape, F32)...  7.59 us

profile of v7, /device:TPU:9, one launch (start us, length us, event | category | flops | bytes accessed | tf_op | source)
XLA Modules:
  0.0 255.6 jit_solution(257467196516460219)
XLA Ops:
  0.6 247.2 %shard_map.179 = (f32[3,128,2048]{2,1,0:T(8,128)S(1)}, f32[3,128,2048]{2,1,0:T(8,128)S(1)}, f32[3,128,1024]{2,1,0:T(8,128)S(1)}, f32[3,128,1024]{2,1,0:T(8,128)S...) custom-call(f32[3,128,2048]{2,1,0:T(8,128)} %w_q.1, ...), custom_call_target="tpu_custom_call" | custom-call | tf_op jit(solution)/shard_map/pallas_call | solution.py:442
  247.9 7.6 %shard_map.180 = (f32[3,128,2048]{2,1,0:T(8,128)}, f32[3,128,2048]{2,1,0:T(8,128)}, f32[3,128,1024]{2,1,0:T(8,128)}, f32[3,128,1024]{2,1,0:T(8,128)}, f32[12,128...) custom-call(f32[3,128,2048]{2,1,0:T(8,128)S(1)} %get-tuple-element.16.refs_0_, ...), custom_call_target="tpu_custom_call" | custom-call | tf_op jit(solution)/shard_map/pallas_call | solution.py:477

commit v8 on v7

--- a/solution.py
+++ b/solution.py
@@ -150,7 +150,7 @@
     def weight_copy(stack, number):
         return pltpu.make_async_copy(weights[stack], new_w[stack], w_sem.at[number])
 
-    for key in loads["o"] + loads["q"]:
+    for key in loads["o"]:
         for copy in load_copies(key):
             copy.start()
 
@@ -253,8 +253,8 @@
 
     for copy in load_copies(("o", None)):
         copy.wait()
-    for stack in ("d", "u"):
-        for copy in load_copies((stack, None)):
+    for key in loads["q"] + loads["d"] + loads["u"]:
+        for copy in load_copies(key):
             copy.start()
     momentum_loop("o", 0)
     pl.semaphore_wait(barrier, GROUP - 1)
@@ -264,9 +264,9 @@
             copy.wait()
         momentum_rows("q", i, 1, i)
     push_norms(1)
-    momentum_stack("d", 2)
     read_norms(0)
     scale_and_send("o", 0)
+    momentum_stack("d", 2)
     momentum_stack("u", 2)
     push_norms(2)
     read_norms(1)

time: 256 us -> 256 us (level)
  no operation moved by 1% of the time
where the time goes in v8:
time: 256 us; the launch traced here: 255 us
  Pallas kernels  255 us (100%)
    pallas_call x1, Pallas kernels, local_step(): pl.pallas_call(kernel, out_shape=[OUT_SPACE(shape, F32) for shape in shap...  247 us
    pallas_call x1, Pallas kernels, local_step(): pl.pallas_call(store_kernel, out_shape=[jax.ShapeDtypeStruct(shape, F32)...  7.59 us

profile of v8, /device:TPU:9, one launch (start us, length us, event | category | flops | bytes accessed | tf_op | source)
XLA Modules:
  0.0 255.5 jit_solution(1814089182493150401)
XLA Ops:
  0.6 247.1 %shard_map.179 = (f32[3,128,2048]{2,1,0:T(8,128)S(1)}, f32[3,128,2048]{2,1,0:T(8,128)S(1)}, f32[3,128,1024]{2,1,0:T(8,128)S(1)}, f32[3,128,1024]{2,1,0:T(8,128)S...) custom-call(f32[3,128,2048]{2,1,0:T(8,128)} %w_q.1, ...), custom_call_target="tpu_custom_call" | custom-call | tf_op jit(solution)/shard_map/pallas_call | solution.py:442
  247.7 7.6 %shard_map.180 = (f32[3,128,2048]{2,1,0:T(8,128)}, f32[3,128,2048]{2,1,0:T(8,128)}, f32[3,128,1024]{2,1,0:T(8,128)}, f32[3,128,1024]{2,1,0:T(8,128)}, f32[12,128...) custom-call(f32[3,128,2048]{2,1,0:T(8,128)S(1)} %get-tuple-element.16.refs_0_, ...), custom_call_target="tpu_custom_call" | custom-call | tf_op jit(solution)/shard_map/pallas_call | solution.py:477

commit v9 on v8

--- a/solution.py
+++ b/solution.py
@@ -95,6 +95,8 @@
 STACKS = {"q": (3, 128, 2048, 32, 0), "o": (3, 128, 1024, 64, 0), "d": (12, 64, 1024, 64, 0), "u": (12, 128, 512, 128, 12)}
 SCALE = {"q": RMS_MATCH * math.sqrt(2048), "o": RMS_MATCH * math.sqrt(1024),
          "d": RMS_MATCH * math.sqrt(1024), "u": RMS_MATCH * math.sqrt(1024)}
+EARLY = {("o", 0): 32, ("o", 1): 32}
+EARLY_ROWS = 32
 SEM_BASE = {"q": 0, "o": 3, "d": 6, "u": 18}
 
 
@@ -123,8 +125,8 @@
 def kernel(w_q, m_q, g_q, w_o, m_o, g_o, w_u, m_u, g_u, w_d, m_d, g_d,
            nw_q, nm_q, nw_o, nm_o, nw_u, nm_u, nw_d, nm_d,
            big, ebuf, gram, poly, xs_q, xs_o, xs_d, xs_u, bk_q, bk_o, bk_d, gs_u, bk_u,
-           part, gath, den,
-           m_sem, g_sem, w_sem, norm_send, norm_recv, fwd_send, fwd_recv, ret_send, ret_recv):
+           part, gath, den, early,
+           m_sem, g_sem, w_sem, norm_send, norm_recv, fwd_send, fwd_recv, ret_send, ret_recv, early_send, early_recv):
     me = lax.axis_index("data")
     weights = {"q": w_q, "o": w_o, "d": w_d, "u": w_u}
     momenta = {"q": m_q, "o": m_o, "d": m_d, "u": m_u}
@@ -216,11 +218,16 @@
     def send_rows(stack, i, owner, slot):
         sem = SEM_BASE[stack] + i
         target = block_of(stack, slot_of(stack, slot), me)
+        skip = EARLY.get((stack, i), 0)
+        source, rest = scaled[stack].at[i], target
+        if skip:
+            source = scaled[stack].at[i, pl.ds(skip, 128 - skip), :]
+            rest = slot_of(stack, slot).at[pl.ds(me * 128 + skip, 128 - skip), :]
 
         @pl.when(me != owner)
         def _():
             pltpu.make_async_remote_copy(
-                src_ref=scaled[stack].at[i], dst_ref=target, send_sem=fwd_send.at[sem], recv_sem=fwd_recv.at[sem],
+                src_ref=source, dst_ref=rest, send_sem=fwd_send.at[sem], recv_sem=fwd_recv.at[sem],
                 device_id={"data": owner}, device_id_type=MESH).start()
 
         @pl.when(me == owner)
@@ -250,6 +257,11 @@
             if kind == stack:
                 scale_rows(stack, i, number, i)
                 send_rows(stack, i, owner, slot)
+
+    def early_copy(i):
+        return pltpu.make_async_remote_copy(
+            src_ref=new_m["o"].at[i, pl.ds(0, EARLY_ROWS), :], dst_ref=early.at[me], send_sem=early_send.at[i],
+            recv_sem=early_recv.at[0], device_id={"data": OUT_OWNER[i]}, device_id_type=MESH)
 
     for copy in load_copies(("o", None)):
         copy.wait()
@@ -259,6 +271,10 @@
     momentum_loop("o", 0)
     pl.semaphore_wait(barrier, GROUP - 1)
     push_norms(0)
+    for i in range(2):
+        @pl.when(me != OUT_OWNER[i])
+        def _():
+            early_copy(i).start()
     for i in range(3):
         for copy in load_copies(("q", i)):
             copy.wait()
@@ -328,7 +344,21 @@
     for index, owner in enumerate(OUT_OWNER):
         @pl.when(me == owner)
         def _():
-            wait_parts("o", big.at[0, :, pl.ds(0, 1024)], fwd_recv.at[3 + index])
+            if ("o", index) not in EARLY:
+                wait_parts("o", big.at[0, :, pl.ds(0, 1024)], fwd_recv.at[3 + index])
+                return
+            part_rows = big.at[0, pl.ds(0, 7 * (128 - EARLY_ROWS)), pl.ds(0, 1024)]
+            pltpu.make_async_copy(part_rows, part_rows, fwd_recv.at[3 + index]).wait()
+            seven = early.at[pl.ds(0, GROUP - 1)]
+            pltpu.make_async_copy(seven, seven, early_recv.at[0]).wait()
+            divisor = jnp.sum(jnp.where(lane[:1] == index, den[0, 0:1, :], 0.0), axis=1, keepdims=True)
+
+            @pl.loop(0, GROUP)
+            def _(d):
+                @pl.when(d != me)
+                def _():
+                    x = early[d] / jnp.broadcast_to(divisor, (EARLY_ROWS, 1024))
+                    big[0, pl.ds(pl.multiple_of(d * 128, 128), EARLY_ROWS), 0:1024] = x.astype(BF16)
 
     @pl.when((me == OUT_OWNER[0]) | (me == OUT_OWNER[1]) | (me == OUT_OWNER[2]))
     def _():
@@ -401,6 +431,9 @@
         @pl.when(me != owner)
         def _():
             block = scaled[stack].at[i]
+            if (stack, i) in EARLY:
+                block = scaled[stack].at[i, pl.ds(EARLY_ROWS, 128 - EARLY_ROWS), :]
+                early_copy(i).wait_send()
             pltpu.make_async_copy(block, block, fwd_send.at[SEM_BASE[stack] + i]).wait()
     for owner in QKV_OWNER:
         @pl.when(me == owner)
@@ -461,6 +494,7 @@
                 pltpu.VMEM((3, 8, 128), F32),
                 pltpu.VMEM((3, GROUP, 8, 128), F32),
                 pltpu.VMEM((3, 8, 128), F32),
+                pltpu.VMEM((GROUP, EARLY_ROWS, 1024), F32),
                 pltpu.SemaphoreType.DMA((6,)),
                 pltpu.SemaphoreType.DMA((6,)),
                 pltpu.SemaphoreType.DMA((4,)),
@@ -470,6 +504,8 @@
                 pltpu.SemaphoreType.DMA((30,)),
                 pltpu.SemaphoreType.DMA((2 + MAX_EXPERTS,)),
                 pltpu.SemaphoreType.DMA((30,)),
+                pltpu.SemaphoreType.DMA((2,)),
+                pltpu.SemaphoreType.DMA((1,)),
             ],
             compiler_params=pltpu.CompilerParams(
                 collective_id=0, has_side_effects=True, vmem_limit_bytes=VMEM_LIMIT),

time: 256 us -> 256 us (level)
  no operation moved by 1% of the time
where the time goes in v9:
time: 256 us; the launch traced here: 255 us
  Pallas kernels  255 us (100%)
    pallas_call x1, Pallas kernels, local_step(): pl.pallas_call(kernel, out_shape=[OUT_SPACE(shape, F32) for shape in shap...  247 us
    pallas_call x1, Pallas kernels, local_step(): pl.pallas_call(store_kernel, out_shape=[jax.ShapeDtypeStruct(shape, F32)...  7.59 us

profile of v9, /device:TPU:9, one launch (start us, length us, event | category | flops | bytes accessed | tf_op | source)
XLA Modules:
  0.0 255.4 jit_solution(715313139420555690)
XLA Ops:
  0.6 247.0 %shard_map.179 = (f32[3,128,2048]{2,1,0:T(8,128)S(1)}, f32[3,128,2048]{2,1,0:T(8,128)S(1)}, f32[3,128,1024]{2,1,0:T(8,128)S(1)}, f32[3,128,1024]{2,1,0:T(8,128)S...) custom-call(f32[3,128,2048]{2,1,0:T(8,128)} %w_q.1, ...), custom_call_target="tpu_custom_call" | custom-call | tf_op jit(solution)/shard_map/pallas_call | solution.py:475
  247.6 7.6 %shard_map.180 = (f32[3,128,2048]{2,1,0:T(8,128)}, f32[3,128,2048]{2,1,0:T(8,128)}, f32[3,128,1024]{2,1,0:T(8,128)}, f32[3,128,1024]{2,1,0:T(8,128)}, f32[12,128...) custom-call(f32[3,128,2048]{2,1,0:T(8,128)S(1)} %get-tuple-element.16.refs_0_, ...), custom_call_target="tpu_custom_call" | custom-call | tf_op jit(solution)/shard_map/pallas_call | solution.py:513

commit v10 on v9

--- a/solution.py
+++ b/solution.py
@@ -22,9 +22,9 @@
 F32 = jnp.float32
 BF16 = jnp.bfloat16
 
-QKV_OWNER = (2, 1, 5)
-OUT_OWNER = (3, 4, 7)
-EXPERT_COUNT = (2, 0, 4, 5, 8, 1, 4, 0)
+QKV_OWNER = (2, 3, 4)
+OUT_OWNER = (0, 5, 6)
+EXPERT_COUNT = (3, 6, 1, 1, 1, 3, 3, 6)
 EXPERT_BASE = tuple(sum(EXPERT_COUNT[:d]) for d in range(GROUP))
 EXPERT_OWNER = tuple(d for d in range(GROUP) for _ in range(EXPERT_COUNT[d]))
 N_DOWN = 12

time: 256 us -> 259 us (1.012)
  Pallas kernels: 255 us -> 258 us
    pallas_call x1, Pallas kernels: 247 us -> 250 us  [local_step(): pl.pallas_call(kernel, out_shape=[OUT_SPACE(shape, F32) for shape in shap...]
where the time goes in v10:
time: 259 us
  Pallas kernels  258 us (100%)
    pallas_call x1, Pallas kernels, local_step(): pl.pallas_call(kernel, out_shape=[OUT_SPACE(shape, F32) for shape in shap...  250 us
    pallas_call x1, Pallas kernels, local_step(): pl.pallas_call(store_kernel, out_shape=[jax.ShapeDtypeStruct(shape, F32)...  7.59 us

profile of v10, /device:TPU:9, one launch (start us, length us, event | category | flops | bytes accessed | tf_op | source)
XLA Modules:
  0.0 258.7 jit_solution(15065783426366327144)
XLA Ops:
  0.6 250.3 %shard_map.179 = (f32[3,128,2048]{2,1,0:T(8,128)S(1)}, f32[3,128,2048]{2,1,0:T(8,128)S(1)}, f32[3,128,1024]{2,1,0:T(8,128)S(1)}, f32[3,128,1024]{2,1,0:T(8,128)S...) custom-call(f32[3,128,2048]{2,1,0:T(8,128)} %w_q.1, ...), custom_call_target="tpu_custom_call" | custom-call | tf_op jit(solution)/shard_map/pallas_call | solution.py:475
  250.9 7.6 %shard_map.180 = (f32[3,128,2048]{2,1,0:T(8,128)}, f32[3,128,2048]{2,1,0:T(8,128)}, f32[3,128,1024]{2,1,0:T(8,128)}, f32[3,128,1024]{2,1,0:T(8,128)}, f32[12,128...) custom-call(f32[3,128,2048]{2,1,0:T(8,128)S(1)} %get-tuple-element.16.refs_0_, ...), custom_call_target="tpu_custom_call" | custom-call | tf_op jit(solution)/shard_map/pallas_call | solution.py:513

commit v11 on v9

--- a/solution.py
+++ b/solution.py
@@ -29,7 +29,7 @@
 EXPERT_OWNER = tuple(d for d in range(GROUP) for _ in range(EXPERT_COUNT[d]))
 N_DOWN = 12
 MAX_EXPERTS = 8
-VMEM_LIMIT = 40 * 1024 * 1024
+VMEM_LIMIT = 42 * 1024 * 1024
 
 
 def send_order():
@@ -365,7 +365,7 @@
         @pl.loop(0, NS_STEPS)
         def _(it):
             now = lax.rem(it, 2)
-            ns_step(big.at[now, :, pl.ds(0, 1024)], big.at[1 - now, :, pl.ds(0, 1024)], gram, poly, 1024, 256)
+            ns_step(big.at[now, :, pl.ds(0, 1024)], big.at[1 - now, :, pl.ds(0, 1024)], gram, poly, 1024, 512)
 
     for index, owner in enumerate(OUT_OWNER):
         @pl.when(me == owner)
@@ -392,7 +392,7 @@
         def _(it):
             src = jnp.where(it == 0, t, MAX_EXPERTS + lax.rem(it + 1, 2))
             dst = jnp.where(it == NS_STEPS - 1, t, MAX_EXPERTS + lax.rem(it, 2))
-            ns_step(ebuf.at[src], ebuf.at[dst], small_gram, small_poly, 512, 256)
+            ns_step(ebuf.at[src], ebuf.at[dst], small_gram, small_poly, 512, 512)
 
         @pl.when(rank < N_DOWN)
         def _():

time: 256 us -> 256 us (level)
  no operation moved by 1% of the time
where the time goes in v11:
time: 256 us; the launch traced here: 255 us
  Pallas kernels  255 us (100%)
    pallas_call x1, Pallas kernels, local_step(): pl.pallas_call(kernel, out_shape=[OUT_SPACE(shape, F32) for shape in shap...  247 us
    pallas_call x1, Pallas kernels, local_step(): pl.pallas_call(store_kernel, out_shape=[jax.ShapeDtypeStruct(shape, F32)...  7.59 us

profile of v11, /device:TPU:9, one launch (start us, length us, event | category | flops | bytes accessed | tf_op | source)
XLA Modules:
  0.0 255.4 jit_solution(7294446831293082958)
XLA Ops:
  0.6 247.0 %shard_map.179 = (f32[3,128,2048]{2,1,0:T(8,128)S(1)}, f32[3,128,2048]{2,1,0:T(8,128)S(1)}, f32[3,128,1024]{2,1,0:T(8,128)S(1)}, f32[3,128,1024]{2,1,0:T(8,128)S...) custom-call(f32[3,128,2048]{2,1,0:T(8,128)} %w_q.1, ...), custom_call_target="tpu_custom_call" | custom-call | tf_op jit(solution)/shard_map/pallas_call | solution.py:475
  247.6 7.6 %shard_map.180 = (f32[3,128,2048]{2,1,0:T(8,128)}, f32[3,128,2048]{2,1,0:T(8,128)}, f32[3,128,1024]{2,1,0:T(8,128)}, f32[3,128,1024]{2,1,0:T(8,128)}, f32[12,128...) custom-call(f32[3,128,2048]{2,1,0:T(8,128)S(1)} %get-tuple-element.16.refs_0_, ...), custom_call_target="tpu_custom_call" | custom-call | tf_op jit(solution)/shard_map/pallas_call | solution.py:513
